TPU v7x, 32 devices: a whole 2x2x4 slice. The times are simulated.
32 devices in a mesh: groups: 2 (over y), dom: 8 (over z, core), tilt: 2 (over x), rep: 1.
Axes of the slice: x: 2, y: 2, z: 4, core: 2. Of those that a mesh axis runs over, the one named last changes fastest.
Arguments:
- patches: bfloat16 [4, 1024, 128, 128], P(('groups', 'tilt'), 'dom'), parts along dimension 0, may hold values from -6 to 6
- slot_view: int32 [4, 1024, 1], P(('groups', 'tilt'), 'dom'), parts along dimension 0, may hold values from 0 to 31, as said below
- slot_tilt: int32 [4, 1024], P(('groups', 'tilt'), 'dom'), parts along dimension 0, may hold values from 0 to 9
- slot_pos: bfloat16 [2, 4, 1024], P(None, ('groups', 'tilt'), 'dom'), parts along dimension 1, may hold values from 0 to 1
- defocus: bfloat16 [4, 1024], P(('groups', 'tilt'), 'dom'), parts along dimension 0, may hold values from 1 to 3
- projections: bfloat16 [64, 20, 2, 128, 128], P(('groups', 'dom'), 'tilt', None, 'rep'), parts along dimension 0, may hold values from -6 to 6
- warp_grid: float32 [40, 2, 256], P(('groups', 'tilt')), parts along dimension 0, may hold values from -6 to 6
Outputs:
- slot_terms: float32 [3, 4, 1024], P(None, ('groups', 'tilt'), 'dom'), parts along dimension 1
- new_warp: float32 [40, 2, 256], P(('groups', 'tilt')), parts along dimension 0
There are 2 independent parts, one for each index of `groups`. A program takes and returns all parts, laid end to end along the dimension named above; each array names one. Nothing has to cross between parts.
Inputs may be any that keep to these rules, and one draw needn't show every extreme that they name: `slot_view`: view v is owned by dom index v // 4. Among the 128 slots of one device (one tilt index and one dom index) at most 24 name views of any one owner, and in every such block some owner is named exactly 24 times.
All inputs are finite; a program needn't handle non-finite values.
Results may differ from a plain program's by a relative error of at most 0.0018.
Values may be sent and summed in bfloat16 or wider, within the bound.
A program may use at most 64 MiB of HBM per device.

v0:
```python
import math

import jax
import jax.numpy as jnp
from jax import lax
from jax.sharding import PartitionSpec as P

GRID = 16


AMPLITUDE = 0.07
TRUST_FLOOR = 0.02


def signed_freq(index, pixels):
    return jnp.where(index < pixels // 2, index, index - pixels).astype(jnp.float32)


def dft_tables(freq_rows, pixels):
    columns = jnp.arange(pixels, dtype=jnp.int32)
    table_scale = 1.0 / math.sqrt(pixels)
    turns_rows = (freq_rows[:, None] * columns[None, :] % pixels).astype(jnp.float32) * (
        2.0 * math.pi / pixels
    )
    turns_full = (columns[:, None] * columns[None, :] % pixels).astype(jnp.float32) * (
        2.0 * math.pi / pixels
    )
    row_table = jnp.concatenate([jnp.cos(turns_rows), jnp.sin(turns_rows)], axis=0) * table_scale
    col_table = jnp.concatenate([jnp.cos(turns_full), jnp.sin(turns_full)], axis=1) * table_scale
    return (row_table.astype(jnp.bfloat16), col_table.astype(jnp.bfloat16))


def node_weights(pos_x, pos_y, grid_side):
    knot_pos = jnp.arange(grid_side, dtype=jnp.int32).astype(jnp.float32)
    weight_x = jnp.maximum(0.0, 1.0 - jnp.abs(pos_x[:, None] * (grid_side - 1) - knot_pos[None, :]))
    weight_y = jnp.maximum(0.0, 1.0 - jnp.abs(pos_y[:, None] * (grid_side - 1) - knot_pos[None, :]))
    return (weight_y[:, :, None] * weight_x[:, None, :]).reshape(
        pos_x.shape[0], grid_side * grid_side
    )


def spectral_terms(spectrum, ref_blk, focus_blk, shift_blk, freq_rows, pixels):
    row_total = freq_rows.shape[0]
    v_one_cos = spectrum[:, :row_total, :pixels]
    v_one_sin = spectrum[:, :row_total, pixels:]
    v_two_cos = spectrum[:, row_total:, :pixels]
    v_two_sin = spectrum[:, row_total:, pixels:]
    real_part = v_one_cos - v_two_sin
    imag_part = -(v_one_sin + v_two_cos)
    freq_y = signed_freq(freq_rows, pixels)[None, :, None]
    freq_x = signed_freq(jnp.arange(pixels, dtype=jnp.int32), pixels)[None, None, :]
    nyquist = pixels / 2.0
    radius = (freq_y * freq_y + freq_x * freq_x) / (nyquist * nyquist)
    aberration = math.pi * focus_blk[:, None, None] * radius
    contrast = -(
        math.sqrt(1.0 - AMPLITUDE * AMPLITUDE) * jnp.sin(aberration)
        + AMPLITUDE * jnp.cos(aberration)
    )
    phase_angle = (
        2.0
        * math.pi
        / pixels
        * (freq_x * shift_blk[:, 0, None, None] + freq_y * shift_blk[:, 1, None, None])
    )
    cosine = jnp.cos(phase_angle)
    sine_part = jnp.sin(phase_angle)
    ref_real = ref_blk[:, 0].astype(jnp.float32)
    ref_imag = ref_blk[:, 1].astype(jnp.float32)
    model_real = contrast * (ref_real * cosine + ref_imag * sine_part)
    model_imag = contrast * (ref_imag * cosine - ref_real * sine_part)
    diff_real = real_part - model_real
    diff_imag = imag_part - model_imag
    inverse_area = 1.0 / (pixels * pixels)
    energy = jnp.sum(diff_real * diff_real + diff_imag * diff_imag, axis=(1, 2)) * inverse_area
    cross_term = diff_imag * model_real - diff_real * model_imag
    grad_x = 2.0 * inverse_area * jnp.sum(2.0 * math.pi / pixels * freq_x * cross_term, axis=(1, 2))
    grad_y = 2.0 * inverse_area * jnp.sum(2.0 * math.pi / pixels * freq_y * cross_term, axis=(1, 2))
    return jnp.stack([energy, grad_x, grad_y], axis=1)


def on_device(patches, slot_view, slot_tilt, slot_pos, defocus, projections, warp_grid):
    owners = lax.axis_size("dom")
    slot_count = patches.shape[1]
    pixels = patches.shape[-1]
    view_dev = projections.shape[0]
    tilt_dev = warp_grid.shape[0]
    node_count = warp_grid.shape[2]
    capacity = 3 * slot_count // (2 * owners)
    buffer_len = owners * capacity
    chosen_view = slot_view[0, :, 0]
    owner_of = chosen_view // view_dev
    owner_hits = (owner_of[:, None] == jnp.arange(owners, dtype=jnp.int32)[None, :]).astype(
        jnp.int32
    )
    earlier = jnp.cumsum(owner_hits, axis=0) - owner_hits
    slot_rank = jnp.sum(earlier * owner_hits, axis=1)
    target = owner_of * capacity + slot_rank
    matches = target[None, :] == jnp.arange(buffer_len, dtype=jnp.int32)[:, None]
    source = jnp.sum(
        jnp.where(matches, jnp.arange(slot_count, dtype=jnp.int32)[None, :], 0), axis=1
    )
    filled = jnp.any(matches, axis=1)
    patch_rows = jnp.where(filled[:, None, None], patches[0][source], jnp.zeros((), jnp.bfloat16))
    slot_meta = jnp.stack(
        [
            slot_tilt[0].astype(jnp.float32),
            (chosen_view % view_dev).astype(jnp.float32),
            defocus[0].astype(jnp.float32),
            slot_pos[0, 0].astype(jnp.float32),
            slot_pos[1, 0].astype(jnp.float32),
            jnp.ones((slot_count,), jnp.float32),
        ],
        axis=1,
    )
    meta_rows = jnp.where(filled[:, None], slot_meta[source], 0.0).astype(jnp.bfloat16)
    patch_buffer = patch_rows.reshape(owners, capacity, pixels, pixels)
    meta_buffer = meta_rows.reshape(owners, capacity, 6)
    row_span = projections.shape[3]
    freq_rows = lax.axis_index("rep") * row_span + jnp.arange(row_span, dtype=jnp.int32)
    row_table, col_table = dft_tables(freq_rows, pixels)
    row_total = freq_rows.shape[0]
    projected_flat = projections.reshape(view_dev * tilt_dev, 2, row_total, pixels)
    tilt_iota = jnp.arange(tilt_dev, dtype=jnp.int32)
    view_iota = jnp.arange(view_dev, dtype=jnp.int32)

    def one_block(inputs):
        patch_blk, index_blk, focus_blk, shift_blk = inputs
        ref_blk = projected_flat[index_blk]
        first_pass = jnp.einsum(
            "fy,byx->bfx", row_table, patch_blk, preferred_element_type=jnp.float32
        ).astype(jnp.bfloat16)
        spectrum = jnp.einsum(
            "bfx,xk->bfk", first_pass, col_table, preferred_element_type=jnp.float32
        )
        return spectral_terms(spectrum, ref_blk, focus_blk, shift_blk, freq_rows, pixels)

    patch_in = lax.all_to_all(patch_buffer, "dom", split_axis=0, concat_axis=0, tiled=True)
    meta_in = lax.all_to_all(meta_buffer, "dom", split_axis=0, concat_axis=0, tiled=True)
    senders = patch_in.shape[0]
    per_sender = patch_in.shape[1]
    slot_total = senders * per_sender
    meta_flat = meta_in.reshape(slot_total, 6).astype(jnp.float32)
    tilt_match = meta_flat[:, 0:1] == tilt_iota.astype(jnp.float32)[None, :]
    view_match = meta_flat[:, 1:2] == view_iota.astype(jnp.float32)[None, :]
    tilt_local = jnp.sum(jnp.where(tilt_match, tilt_iota[None, :], 0), axis=1)
    view_local = jnp.sum(jnp.where(view_match, view_iota[None, :], 0), axis=1)
    weights = node_weights(meta_flat[:, 3], meta_flat[:, 4], GRID)
    shifts = jnp.sum(warp_grid[tilt_local] * weights[:, None, :], axis=2)
    block_len = math.gcd(slot_total, 16)
    block_count = slot_total // block_len
    per_slot = lax.map(
        one_block,
        (
            patch_in.reshape(block_count, block_len, pixels, pixels),
            (view_local * tilt_dev + tilt_local).reshape(block_count, block_len),
            meta_flat[:, 2].reshape(block_count, block_len),
            shifts.reshape(block_count, block_len, 2),
        ),
    ).reshape(slot_total, 3)
    node_coef = (
        tilt_match.astype(jnp.float32)[:, :, None]
        * per_slot[:, None, 1:3]
        * meta_flat[:, 5, None, None]
    ).reshape(senders, per_sender, 2 * tilt_dev)
    returned = lax.all_to_all(
        per_slot.reshape(senders, per_sender, 3), "dom", split_axis=0, concat_axis=0, tiled=True
    )
    weight_all = weights.reshape(senders, per_sender, node_count)
    own_terms = returned.reshape(buffer_len, 3)[target]
    summed = lax.psum(own_terms, "rep")
    slot_terms = summed.T[:, None, :]
    gradient = jnp.dot(
        node_coef.reshape(-1, 2 * tilt_dev).T,
        weight_all.reshape(-1, node_count),
        precision=lax.Precision.HIGHEST,
        preferred_element_type=jnp.float32,
    ).reshape(tilt_dev, 2, node_count)
    whole_grad = lax.psum(gradient, ("dom", "rep"))
    new_warp = warp_grid - whole_grad / jnp.sqrt(
        whole_grad * whole_grad + TRUST_FLOOR * TRUST_FLOOR
    )
    return (slot_terms, new_warp)


def solution(mesh):
    in_specs = (
        P(("groups", "tilt"), "dom", None, None),
        P(("groups", "tilt"), "dom", None),
        P(("groups", "tilt"), "dom"),
        P(None, ("groups", "tilt"), "dom"),
        P(("groups", "tilt"), "dom"),
        P(("groups", "dom"), "tilt", None, "rep", None),
        P(("groups", "tilt"), None, None),
    )
    out_specs = (P(None, ("groups", "tilt"), "dom"), P(("groups", "tilt"), None, None))
    return jax.shard_map(
        on_device, mesh=mesh, in_specs=in_specs, out_specs=out_specs, check_vma=False
    )
```

profile of v0, /device:TPU:0, one launch (start us, length us, event | category | flops | bytes accessed | tf_op | source)
XLA Modules:
  0.0 444.6 jit_solution(1007006649997248516)
XLA Ops:
  5.6 0.8 gather_fusion.2
  7.2 6.4 %all-to-all-start.1 = ((bf16[8,24,6]{1,2,0:T(8,128)(2,1)}), bf16[8,24,6]{1,2,0:T(8,128)(2,1)S(1)}, u32[]{:S(2)}, u32[]{:S(2)}) async-start(bf16[8,24,6]{1,2,0:T(8,128)(2,1)} %select_convert_fusion), calls=%async_computation.1 | async-start | bytes 32768 | tf_op jit(solution)/shard_map/all_to_all | solution.py:138
  13.5 10.2 %gather_fusion.1 = bf16[192,128,128]{2,1,0:T(8,128)(2,1)} fusion(bf16[128,128,128]{2,1,0:T(8,128)(2,1)} %bitcast.181, s32[1024]{0:T(1024)S(1)} %pad_clamp_fusion.3), kind=kCustom, calls=%fused_computation.1 | custom fusion | bytes 12583680 | tf_op jit(solution)/shard_map/gather | solution.py:103
  23.8 8.6 %copy.103 = bf16[8,24,128,128]{2,3,1,0:T(8,128)(2,1)} copy(bf16[8,24,128,128]{3,2,1,0:T(8,128)(2,1)} %bitcast.179) | data formatting | bytes 12582912 | tf_op jit(solution)/shard_map/gather | solution.py:103
  32.4 5.9 %broadcast_select_fusion = bf16[8,24,128,128]{2,3,1,0:T(8,128)(2,1)} fusion(bf16[8,24,128,128]{2,3,1,0:T(8,128)(2,1)} %copy.103, pred[8,24]{1,0:T(8,128)(4,1)S(1)} %broadcast_in_dim.106), kind=kLoop, calls=%fused_computation.65 | loop fusion | flops 3145728 | bytes 12583104 | tf_op jit(solution)/shard_map/jit(_where)/select_n | solution.py:103
  38.3 5.2 %all-to-all-start = ((bf16[8,24,128,128]{2,3,1,0:T(8,128)(2,1)}), bf16[8,24,128,128]{2,3,1,0:T(8,128)(2,1)}, u32[]{:S(2)}, u32[]{:S(2)}) async-start(bf16[8,24,128,128]{2,3,1,0:T(8,128)(2,1)} %broadcast_select_fusion), calls=%async_computation | async-start | bytes 12582912 | tf_op jit(solution)/shard_map/all_to_all | solution.py:137
  44.4 1.1 gather_fusion.3
  46.2 136.3 %all-to-all-done = bf16[8,24,128,128]{2,3,1,0:T(8,128)(2,1)} async-done(((bf16[8,24,128,128]{2,3,1,0:T(8,128)(2,1)}), bf16[8,24,128,128]{2,3,1,0:T(8,128)(2,1)}, u32[]{:S(2)}, u32[]{:S(2)}) %all-to-all-start) | async-done | bytes 6291488 | tf_op jit(solution)/shard_map/all_to_all | solution.py:137
  182.6 223.7 %while.15 = (s32[]{:T(128)}, f32[12,16,3]{1,0,2:T(8,128)S(1)}, bf16[12,16,128,128]{2,3,1,0:T(8,128)(2,1)}, bf16[256,128]{1,0:T(8,128)(2,1)S(1)}, bf16[128,256]{1...) while((s32[]{:T(128)}, f32[12,16,3]{1,0,2:T(8,128)S(1)}, ...), condition=%wide.region_11.12_spmd.clone.clone, body=%wide.region_7.11_spmd.clone.clone.sunk | while | flops 411868064 | bytes 14461309 | solution.py:151
  182.7 4.5 %fusion.62 = f32[16,256,256]{2,1,0:T(8,128)} fusion(bf16[12,16,128,128]{2,3,1,0:T(8,128)(2,1)} %get-tuple-element.403, s32[]{:T(128)} %get-tuple-element.390, bf16[128,256]{1,0:T(8,128)(2,1)S(1)} %get-tuple-element.405, bf16[256,128]{1,0:T(8,128)(2,1)S(1)} %get-tuple-element.404), kind=kOutput, calls=%fused_computation.10.clone.1 | convolution fusion | flops 403177472 | bytes 4850176 | tf_op jit(solution)/shard_map/while/body/eval_jaxpr/bfx,xk->bfk/dot_general | solution.py:132
  187.2 2.5 gather_fusion
  189.8 10.9 %add_reduce_fusion.2 = (f32[16]{0:T(128)S(1)}, f32[16,128,128]{2,1,0:T(8,128)S(1)}) fusion(f32[16,256,256]{2,1,0:T(8,128)} %fusion.62, bf16[16,2,128,128]{3,2,1,0:T(8,128)(2,1)S(1)} %gather_fusion, f32[16,128]{1,0:T(8,128)S(1)} %get-tuple-element.371, f32[16,128]{1,0:T(8,128)S(1)} %get-tuple-element.372, f32[128,128]{1,0:T(8,128)S(1)} %add_multiply_fusion.3, ...), kind=kLoop, calls=%fused_computation.31.clone.1 | loop fusion | flops 7602160 | bytes 6373504 | tf_op jit(solution)/shard_map/while/body/eval_jaxpr/reduce_sum | solution.py:74
  201.3 4.5 %fusion.62 = f32[16,256,256]{2,1,0:T(8,128)} fusion(bf16[12,16,128,128]{2,3,1,0:T(8,128)(2,1)} %get-tuple-element.403, s32[]{:T(128)} %get-tuple-element.390, bf16[128,256]{1,0:T(8,128)(2,1)S(1)} %get-tuple-element.405, bf16[256,128]{1,0:T(8,128)(2,1)S(1)} %get-tuple-element.404), kind=kOutput, calls=%fused_computation.10.clone.1 | convolution fusion | flops 403177472 | bytes 4850176 | tf_op jit(solution)/shard_map/while/body/eval_jaxpr/bfx,xk->bfk/dot_general | solution.py:132
  205.9 2.5 gather_fusion
  208.5 10.9 %add_reduce_fusion.2 = (f32[16]{0:T(128)S(1)}, f32[16,128,128]{2,1,0:T(8,128)S(1)}) fusion(f32[16,256,256]{2,1,0:T(8,128)} %fusion.62, bf16[16,2,128,128]{3,2,1,0:T(8,128)(2,1)S(1)} %gather_fusion, f32[16,128]{1,0:T(8,128)S(1)} %get-tuple-element.371, f32[16,128]{1,0:T(8,128)S(1)} %get-tuple-element.372, f32[128,128]{1,0:T(8,128)S(1)} %add_multiply_fusion.3, ...), kind=kLoop, calls=%fused_computation.31.clone.1 | loop fusion | flops 7602160 | bytes 6373504 | tf_op jit(solution)/shard_map/while/body/eval_jaxpr/reduce_sum | solution.py:74
  220.0 4.5 %fusion.62 = f32[16,256,256]{2,1,0:T(8,128)} fusion(bf16[12,16,128,128]{2,3,1,0:T(8,128)(2,1)} %get-tuple-element.403, s32[]{:T(128)} %get-tuple-element.390, bf16[128,256]{1,0:T(8,128)(2,1)S(1)} %get-tuple-element.405, bf16[256,128]{1,0:T(8,128)(2,1)S(1)} %get-tuple-element.404), kind=kOutput, calls=%fused_computation.10.clone.1 | convolution fusion | flops 403177472 | bytes 4850176 | tf_op jit(solution)/shard_map/while/body/eval_jaxpr/bfx,xk->bfk/dot_general | solution.py:132
  224.5 2.5 gather_fusion
  227.1 10.9 %add_reduce_fusion.2 = (f32[16]{0:T(128)S(1)}, f32[16,128,128]{2,1,0:T(8,128)S(1)}) fusion(f32[16,256,256]{2,1,0:T(8,128)} %fusion.62, bf16[16,2,128,128]{3,2,1,0:T(8,128)(2,1)S(1)} %gather_fusion, f32[16,128]{1,0:T(8,128)S(1)} %get-tuple-element.371, f32[16,128]{1,0:T(8,128)S(1)} %get-tuple-element.372, f32[128,128]{1,0:T(8,128)S(1)} %add_multiply_fusion.3, ...), kind=kLoop, calls=%fused_computation.31.clone.1 | loop fusion | flops 7602160 | bytes 6373504 | tf_op jit(solution)/shard_map/while/body/eval_jaxpr/reduce_sum | solution.py:74
  238.6 4.5 %fusion.62 = f32[16,256,256]{2,1,0:T(8,128)} fusion(bf16[12,16,128,128]{2,3,1,0:T(8,128)(2,1)} %get-tuple-element.403, s32[]{:T(128)} %get-tuple-element.390, bf16[128,256]{1,0:T(8,128)(2,1)S(1)} %get-tuple-element.405, bf16[256,128]{1,0:T(8,128)(2,1)S(1)} %get-tuple-element.404), kind=kOutput, calls=%fused_computation.10.clone.1 | convolution fusion | flops 403177472 | bytes 4850176 | tf_op jit(solution)/shard_map/while/body/eval_jaxpr/bfx,xk->bfk/dot_general | solution.py:132
  243.1 2.5 gather_fusion
  245.8 10.9 %add_reduce_fusion.2 = (f32[16]{0:T(128)S(1)}, f32[16,128,128]{2,1,0:T(8,128)S(1)}) fusion(f32[16,256,256]{2,1,0:T(8,128)} %fusion.62, bf16[16,2,128,128]{3,2,1,0:T(8,128)(2,1)S(1)} %gather_fusion, f32[16,128]{1,0:T(8,128)S(1)} %get-tuple-element.371, f32[16,128]{1,0:T(8,128)S(1)} %get-tuple-element.372, f32[128,128]{1,0:T(8,128)S(1)} %add_multiply_fusion.3, ...), kind=kLoop, calls=%fused_computation.31.clone.1 | loop fusion | flops 7602160 | bytes 6373504 | tf_op jit(solution)/shard_map/while/body/eval_jaxpr/reduce_sum | solution.py:74
  257.3 4.5 %fusion.62 = f32[16,256,256]{2,1,0:T(8,128)} fusion(bf16[12,16,128,128]{2,3,1,0:T(8,128)(2,1)} %get-tuple-element.403, s32[]{:T(128)} %get-tuple-element.390, bf16[128,256]{1,0:T(8,128)(2,1)S(1)} %get-tuple-element.405, bf16[256,128]{1,0:T(8,128)(2,1)S(1)} %get-tuple-element.404), kind=kOutput, calls=%fused_computation.10.clone.1 | convolution fusion | flops 403177472 | bytes 4850176 | tf_op jit(solution)/shard_map/while/body/eval_jaxpr/bfx,xk->bfk/dot_general | solution.py:132
  261.8 2.5 gather_fusion
  264.4 10.9 %add_reduce_fusion.2 = (f32[16]{0:T(128)S(1)}, f32[16,128,128]{2,1,0:T(8,128)S(1)}) fusion(f32[16,256,256]{2,1,0:T(8,128)} %fusion.62, bf16[16,2,128,128]{3,2,1,0:T(8,128)(2,1)S(1)} %gather_fusion, f32[16,128]{1,0:T(8,128)S(1)} %get-tuple-element.371, f32[16,128]{1,0:T(8,128)S(1)} %get-tuple-element.372, f32[128,128]{1,0:T(8,128)S(1)} %add_multiply_fusion.3, ...), kind=kLoop, calls=%fused_computation.31.clone.1 | loop fusion | flops 7602160 | bytes 6373504 | tf_op jit(solution)/shard_map/while/body/eval_jaxpr/reduce_sum | solution.py:74
  275.9 4.5 %fusion.62 = f32[16,256,256]{2,1,0:T(8,128)} fusion(bf16[12,16,128,128]{2,3,1,0:T(8,128)(2,1)} %get-tuple-element.403, s32[]{:T(128)} %get-tuple-element.390, bf16[128,256]{1,0:T(8,128)(2,1)S(1)} %get-tuple-element.405, bf16[256,128]{1,0:T(8,128)(2,1)S(1)} %get-tuple-element.404), kind=kOutput, calls=%fused_computation.10.clone.1 | convolution fusion | flops 403177472 | bytes 4850176 | tf_op jit(solution)/shard_map/while/body/eval_jaxpr/bfx,xk->bfk/dot_general | solution.py:132
  280.4 2.5 gather_fusion
  283.1 10.9 %add_reduce_fusion.2 = (f32[16]{0:T(128)S(1)}, f32[16,128,128]{2,1,0:T(8,128)S(1)}) fusion(f32[16,256,256]{2,1,0:T(8,128)} %fusion.62, bf16[16,2,128,128]{3,2,1,0:T(8,128)(2,1)S(1)} %gather_fusion, f32[16,128]{1,0:T(8,128)S(1)} %get-tuple-element.371, f32[16,128]{1,0:T(8,128)S(1)} %get-tuple-element.372, f32[128,128]{1,0:T(8,128)S(1)} %add_multiply_fusion.3, ...), kind=kLoop, calls=%fused_computation.31.clone.1 | loop fusion | flops 7602160 | bytes 6373504 | tf_op jit(solution)/shard_map/while/body/eval_jaxpr/reduce_sum | solution.py:74
  294.6 4.5 %fusion.62 = f32[16,256,256]{2,1,0:T(8,128)} fusion(bf16[12,16,128,128]{2,3,1,0:T(8,128)(2,1)} %get-tuple-element.403, s32[]{:T(128)} %get-tuple-element.390, bf16[128,256]{1,0:T(8,128)(2,1)S(1)} %get-tuple-element.405, bf16[256,128]{1,0:T(8,128)(2,1)S(1)} %get-tuple-element.404), kind=kOutput, calls=%fused_computation.10.clone.1 | convolution fusion | flops 403177472 | bytes 4850176 | tf_op jit(solution)/shard_map/while/body/eval_jaxpr/bfx,xk->bfk/dot_general | solution.py:132
  299.1 2.5 gather_fusion
  301.7 10.9 %add_reduce_fusion.2 = (f32[16]{0:T(128)S(1)}, f32[16,128,128]{2,1,0:T(8,128)S(1)}) fusion(f32[16,256,256]{2,1,0:T(8,128)} %fusion.62, bf16[16,2,128,128]{3,2,1,0:T(8,128)(2,1)S(1)} %gather_fusion, f32[16,128]{1,0:T(8,128)S(1)} %get-tuple-element.371, f32[16,128]{1,0:T(8,128)S(1)} %get-tuple-element.372, f32[128,128]{1,0:T(8,128)S(1)} %add_multiply_fusion.3, ...), kind=kLoop, calls=%fused_computation.31.clone.1 | loop fusion | flops 7602160 | bytes 6373504 | tf_op jit(solution)/shard_map/while/body/eval_jaxpr/reduce_sum | solution.py:74
  313.2 4.5 %fusion.62 = f32[16,256,256]{2,1,0:T(8,128)} fusion(bf16[12,16,128,128]{2,3,1,0:T(8,128)(2,1)} %get-tuple-element.403, s32[]{:T(128)} %get-tuple-element.390, bf16[128,256]{1,0:T(8,128)(2,1)S(1)} %get-tuple-element.405, bf16[256,128]{1,0:T(8,128)(2,1)S(1)} %get-tuple-element.404), kind=kOutput, calls=%fused_computation.10.clone.1 | convolution fusion | flops 403177472 | bytes 4850176 | tf_op jit(solution)/shard_map/while/body/eval_jaxpr/bfx,xk->bfk/dot_general | solution.py:132
  317.7 2.5 gather_fusion
  320.4 10.9 %add_reduce_fusion.2 = (f32[16]{0:T(128)S(1)}, f32[16,128,128]{2,1,0:T(8,128)S(1)}) fusion(f32[16,256,256]{2,1,0:T(8,128)} %fusion.62, bf16[16,2,128,128]{3,2,1,0:T(8,128)(2,1)S(1)} %gather_fusion, f32[16,128]{1,0:T(8,128)S(1)} %get-tuple-element.371, f32[16,128]{1,0:T(8,128)S(1)} %get-tuple-element.372, f32[128,128]{1,0:T(8,128)S(1)} %add_multiply_fusion.3, ...), kind=kLoop, calls=%fused_computation.31.clone.1 | loop fusion | flops 7602160 | bytes 6373504 | tf_op jit(solution)/shard_map/while/body/eval_jaxpr/reduce_sum | solution.py:74
  331.9 4.5 %fusion.62 = f32[16,256,256]{2,1,0:T(8,128)} fusion(bf16[12,16,128,128]{2,3,1,0:T(8,128)(2,1)} %get-tuple-element.403, s32[]{:T(128)} %get-tuple-element.390, bf16[128,256]{1,0:T(8,128)(2,1)S(1)} %get-tuple-element.405, bf16[256,128]{1,0:T(8,128)(2,1)S(1)} %get-tuple-element.404), kind=kOutput, calls=%fused_computation.10.clone.1 | convolution fusion | flops 403177472 | bytes 4850176 | tf_op jit(solution)/shard_map/while/body/eval_jaxpr/bfx,xk->bfk/dot_general | solution.py:132
  336.4 2.5 gather_fusion
  339.0 10.9 %add_reduce_fusion.2 = (f32[16]{0:T(128)S(1)}, f32[16,128,128]{2,1,0:T(8,128)S(1)}) fusion(f32[16,256,256]{2,1,0:T(8,128)} %fusion.62, bf16[16,2,128,128]{3,2,1,0:T(8,128)(2,1)S(1)} %gather_fusion, f32[16,128]{1,0:T(8,128)S(1)} %get-tuple-element.371, f32[16,128]{1,0:T(8,128)S(1)} %get-tuple-element.372, f32[128,128]{1,0:T(8,128)S(1)} %add_multiply_fusion.3, ...), kind=kLoop, calls=%fused_computation.31.clone.1 | loop fusion | flops 7602160 | bytes 6373504 | tf_op jit(solution)/shard_map/while/body/eval_jaxpr/reduce_sum | solution.py:74
  350.5 4.5 %fusion.62 = f32[16,256,256]{2,1,0:T(8,128)} fusion(bf16[12,16,128,128]{2,3,1,0:T(8,128)(2,1)} %get-tuple-element.403, s32[]{:T(128)} %get-tuple-element.390, bf16[128,256]{1,0:T(8,128)(2,1)S(1)} %get-tuple-element.405, bf16[256,128]{1,0:T(8,128)(2,1)S(1)} %get-tuple-element.404), kind=kOutput, calls=%fused_computation.10.clone.1 | convolution fusion | flops 403177472 | bytes 4850176 | tf_op jit(solution)/shard_map/while/body/eval_jaxpr/bfx,xk->bfk/dot_general | solution.py:132
  355.0 2.5 gather_fusion
  357.7 10.9 %add_reduce_fusion.2 = (f32[16]{0:T(128)S(1)}, f32[16,128,128]{2,1,0:T(8,128)S(1)}) fusion(f32[16,256,256]{2,1,0:T(8,128)} %fusion.62, bf16[16,2,128,128]{3,2,1,0:T(8,128)(2,1)S(1)} %gather_fusion, f32[16,128]{1,0:T(8,128)S(1)} %get-tuple-element.371, f32[16,128]{1,0:T(8,128)S(1)} %get-tuple-element.372, f32[128,128]{1,0:T(8,128)S(1)} %add_multiply_fusion.3, ...), kind=kLoop, calls=%fused_computation.31.clone.1 | loop fusion | flops 7602160 | bytes 6373504 | tf_op jit(solution)/shard_map/while/body/eval_jaxpr/reduce_sum | solution.py:74
  369.2 4.5 %fusion.62 = f32[16,256,256]{2,1,0:T(8,128)} fusion(bf16[12,16,128,128]{2,3,1,0:T(8,128)(2,1)} %get-tuple-element.403, s32[]{:T(128)} %get-tuple-element.390, bf16[128,256]{1,0:T(8,128)(2,1)S(1)} %get-tuple-element.405, bf16[256,128]{1,0:T(8,128)(2,1)S(1)} %get-tuple-element.404), kind=kOutput, calls=%fused_computation.10.clone.1 | convolution fusion | flops 403177472 | bytes 4850176 | tf_op jit(solution)/shard_map/while/body/eval_jaxpr/bfx,xk->bfk/dot_general | solution.py:132
  373.7 2.5 gather_fusion
  376.3 10.9 %add_reduce_fusion.2 = (f32[16]{0:T(128)S(1)}, f32[16,128,128]{2,1,0:T(8,128)S(1)}) fusion(f32[16,256,256]{2,1,0:T(8,128)} %fusion.62, bf16[16,2,128,128]{3,2,1,0:T(8,128)(2,1)S(1)} %gather_fusion, f32[16,128]{1,0:T(8,128)S(1)} %get-tuple-element.371, f32[16,128]{1,0:T(8,128)S(1)} %get-tuple-element.372, f32[128,128]{1,0:T(8,128)S(1)} %add_multiply_fusion.3, ...), kind=kLoop, calls=%fused_computation.31.clone.1 | loop fusion | flops 7602160 | bytes 6373504 | tf_op jit(solution)/shard_map/while/body/eval_jaxpr/reduce_sum | solution.py:74
  387.8 4.5 %fusion.62 = f32[16,256,256]{2,1,0:T(8,128)} fusion(bf16[12,16,128,128]{2,3,1,0:T(8,128)(2,1)} %get-tuple-element.403, s32[]{:T(128)} %get-tuple-element.390, bf16[128,256]{1,0:T(8,128)(2,1)S(1)} %get-tuple-element.405, bf16[256,128]{1,0:T(8,128)(2,1)S(1)} %get-tuple-element.404), kind=kOutput, calls=%fused_computation.10.clone.1 | convolution fusion | flops 403177472 | bytes 4850176 | tf_op jit(solution)/shard_map/while/body/eval_jaxpr/bfx,xk->bfk/dot_general | solution.py:132
  392.3 2.5 gather_fusion
  395.0 10.9 %add_reduce_fusion.2 = (f32[16]{0:T(128)S(1)}, f32[16,128,128]{2,1,0:T(8,128)S(1)}) fusion(f32[16,256,256]{2,1,0:T(8,128)} %fusion.62, bf16[16,2,128,128]{3,2,1,0:T(8,128)(2,1)S(1)} %gather_fusion, f32[16,128]{1,0:T(8,128)S(1)} %get-tuple-element.371, f32[16,128]{1,0:T(8,128)S(1)} %get-tuple-element.372, f32[128,128]{1,0:T(8,128)S(1)} %add_multiply_fusion.3, ...), kind=kLoop, calls=%fused_computation.31.clone.1 | loop fusion | flops 7602160 | bytes 6373504 | tf_op jit(solution)/shard_map/while/body/eval_jaxpr/reduce_sum | solution.py:74
  406.9 26.7 %psum.6 = f32[10,2,256]{2,0,1:T(8,128)S(1)} all-reduce(f32[10,2,256]{2,0,1:T(8,128)S(1)} %fusion.42), channel_id=1, replica_groups=mesh['groups'=2,'dom'=8,'tilt'=2,'rep'=1] {'dom','rep'}, use_global_device_ids=true, to_apply=%region_12.13 | all-reduce | flops 5120 | bytes 40960 | tf_op jit(solution)/shard_map/psum | solution.py:178
  434.3 3.3 all-to-all-start.2
  438.3 4.9 %all-to-all-done.2 = f32[8,24,3]{1,2,0:T(4,128)S(1)} async-done(((f32[8,24,3]{1,2,0:T(4,128)}), f32[8,24,3]{1,2,0:T(4,128)S(1)}, u32[]{:S(2)}, u32[]{:S(2)}) %all-to-all-start.2) | async-done | bytes 2336 | tf_op jit(solution)/shard_map/all_to_all | solution.py:165
  (251 shorter events, 17.9 us)
Async XLA Ops:
  7.2 31.1 %all-to-all-start.1 = ((bf16[8,24,6]{1,2,0:T(8,128)(2,1)}), bf16[8,24,6]{1,2,0:T(8,128)(2,1)S(1)}, u32[]{:S(2)}, u32[]{:S(2)}) async-start(bf16[8,24,6]{1,2,0:T(8,128)(2,1)} %select_convert_fusion), calls=%async_computation.1 | async-start | bytes 32768 | tf_op jit(solution)/shard_map/all_to_all | solution.py:138
  38.3 6.1 %copy-start = (f32[10,2,256]{2,1,0:T(2,128)S(1)}, f32[10,2,256]{2,1,0:T(2,128)}, u32[]{:S(2)}) copy-start(f32[10,2,256]{2,1,0:T(2,128)} %param.15) | copy-start | bytes 61444
  38.3 144.3 %all-to-all-start = ((bf16[8,24,128,128]{2,3,1,0:T(8,128)(2,1)}), bf16[8,24,128,128]{2,3,1,0:T(8,128)(2,1)}, u32[]{:S(2)}, u32[]{:S(2)}) async-start(bf16[8,24,128,128]{2,3,1,0:T(8,128)(2,1)} %broadcast_select_fusion), calls=%async_computation | async-start | bytes 12582912 | tf_op jit(solution)/shard_map/all_to_all | solution.py:137
  434.3 8.9 %all-to-all-start.2 = ((f32[8,24,3]{1,2,0:T(4,128)}), f32[8,24,3]{1,2,0:T(4,128)S(1)}, u32[]{:S(2)}, u32[]{:S(2)}) async-start(f32[8,24,3]{1,2,0:T(4,128)} %copy.111), calls=%async_computation.2 | async-start | bytes 32768 | tf_op jit(solution)/shard_map/all_to_all | solution.py:165
where the time goes:
time: 447 us; the launch traced here: 445 us
  other arithmetic  149 us (33%)
  waiting for transfers between devices  141 us (32%)
  local copies, waits for them, and re-layouts  56.4 us (13%)
  matrix products  54.4 us (12%)
  blocking collectives  26.7 us (6%)
  starting transfers between devices  14.9 us (3%)
    all_to_all x1, waiting for transfers between devices, on_device(): lax.all_to_all(patch_buffer, 'dom', split_axis=0, concat_axis=0, tiled=True)  136 us
    reduce_sum x12, other arithmetic, spectral_terms(): jnp.sum(diff_real * diff_real + diff_imag * diff_imag, axis=(1, 2))  131 us
    dot_general x12, matrix products, one_block(): jnp.einsum('bfx,xk->bfk', first_pass, col_table, preferred_element_type=j...  54.1 us
    gather x12, local copies, waits for them, and re-layouts, one_block(): ref_blk = projected_flat[index_blk]  29.9 us
    psum x1, blocking collectives, on_device(): whole_grad = lax.psum(gradient, ('dom', 'rep'))  26.7 us
    gather x2, local copies, waits for them, and re-layouts, on_device(): patches[0][source]  18.8 us
  transfers between devices with their start and end apart: 3, of which 2 were waited for; matrix products, arithmetic and copies ran while one was open for 6% of the time, Pallas kernels for 0%

commit v1 on v0

--- a/solution.py
+++ b/solution.py
@@ -1,8 +1,11 @@
+import functools
 import math
 
 import jax
 import jax.numpy as jnp
 from jax import lax
+from jax.experimental import pallas as pl
+from jax.experimental.pallas import tpu as pltpu
 from jax.sharding import PartitionSpec as P
 
 GRID = 16
@@ -182,7 +185,372 @@
     return (slot_terms, new_warp)
 
 
+CORES = 2
+EXTRA_ROWS = 8
+RANK = 16
+DELTA = math.asin(AMPLITUDE)
+F32 = jnp.float32
+BF16 = jnp.bfloat16
+
+
+def two_parts(values):
+    high = values.astype(BF16)
+    return high, (values - high.astype(F32)).astype(BF16)
+
+
+def fold_references(projections, pixels):
+    half = pixels // 2
+    refs = projections.reshape(-1, 2, pixels, pixels)
+    k = jnp.arange(pixels, dtype=jnp.int32)
+    lane_freq = k % half
+    lane_part = k // half
+    chan = jnp.arange(2, dtype=jnp.int32)
+    same_part = chan[:, None, None] == lane_part[None, None, :]
+    pick = (same_part & (k[None, :, None] == lane_freq[None, None, :])).astype(BF16)
+    flip = (
+        same_part
+        & (k[None, :, None] == pixels - lane_freq[None, None, :])
+        & (lane_freq > 0)[None, None, :]
+    ).astype(BF16)
+    rows_flip = ((k[:, None] + k[None, :]) % pixels == 0) & (k != half)[:, None]
+    straight = jnp.einsum("ncyx,cxl->nyl", refs, pick, preferred_element_type=F32)
+    mirrored = jnp.einsum("ncyx,cxl->nyl", refs, flip, preferred_element_type=F32).astype(BF16)
+    turned = jnp.einsum("zy,nyl->nzl", rows_flip.astype(BF16), mirrored, preferred_element_type=F32)
+    sign = jnp.where(lane_part == 0, 1.0, -1.0)
+    packed = (straight + sign * turned).astype(BF16)
+    column = refs[:, :, :, half]
+    right = mirrored[:, half : half + 1, :]
+    table = jnp.arange(2 * pixels, dtype=jnp.int32)
+    focus = jnp.where(
+        table < pixels, 1.0 + table / pixels, 2.0 + (table - pixels) / (pixels // 2)
+    ).astype(F32)
+    freq = signed_freq(k, pixels)
+    chi = math.pi * focus[None, :] * (freq * freq / (half * half))[:, None]
+    real = refs[:, 0].astype(F32)
+    imag = refs[:, 1].astype(F32)
+    power = real * real + imag * imag
+    waves = jnp.concatenate([jnp.cos(2.0 * chi), jnp.sin(2.0 * chi)], axis=1).astype(BF16)
+    mixed = jnp.einsum("nyx,xd->nyd", power.astype(BF16), waves, preferred_element_type=F32)
+    turn = 2.0 * chi + 2.0 * DELTA
+    weights = jnp.concatenate([jnp.cos(turn), -jnp.sin(turn)], axis=1)
+    swing = jnp.sum(mixed * weights[None], axis=1)
+    swing = swing[:, : 2 * pixels] + swing[:, 2 * pixels :]
+    total = 0.5 * jnp.sum(power, axis=(1, 2))[:, None] - 0.5 * swing
+    high, low = two_parts(total)
+    count = refs.shape[0]
+    extra = jnp.concatenate(
+        [
+            column,
+            right,
+            high.reshape(count, 2, pixels),
+            low.reshape(count, 2, pixels),
+            jnp.zeros((count, EXTRA_ROWS - 7, pixels), BF16),
+        ],
+        axis=1,
+    )
+    return jnp.concatenate([packed, extra], axis=1)
+
+
+def line_gather_kernel(chips, own_ref, all_ref, right_send, right_recv, left_send, left_recv,
+                       pair_send, pair_recv, local_sem):
+    me = lax.axis_index("dom")
+    chip = me // CORES
+    core = me % CORES
+    partner = chip * CORES + (1 - core)
+    right = me + CORES
+    left = me - CORES
+    last = chips - 1
+    barrier = pltpu.get_barrier_semaphore()
+
+    def greet(device):
+        pl.semaphore_signal(
+            barrier, inc=1, device_id={"dom": device}, device_id_type=pl.DeviceIdType.MESH
+        )
+
+    greet(partner)
+
+    @pl.when(chip < last)
+    def _():
+        greet(right)
+
+    @pl.when(chip > 0)
+    def _():
+        greet(left)
+
+    inner = (chip > 0) & (chip < last)
+
+    @pl.when(inner)
+    def _():
+        pl.semaphore_wait(barrier, 3)
+
+    @pl.when(jnp.logical_not(inner))
+    def _():
+        pl.semaphore_wait(barrier, 2)
+
+    def copy(src, owner, send, recv, target):
+        return pltpu.make_async_remote_copy(
+            src_ref=src, dst_ref=all_ref.at[owner], send_sem=send, recv_sem=recv,
+            device_id={"dom": target}, device_id_type=pl.DeviceIdType.MESH,
+        )
+
+    def to_right(src, hop):
+        return copy(src, me - CORES * hop, right_send.at[hop], right_recv.at[hop], right)
+
+    def to_left(src, hop):
+        return copy(src, me + CORES * hop, left_send.at[hop], left_recv.at[hop], left)
+
+    def to_pair(src, owner):
+        slot = owner // CORES
+        return copy(src, owner, pair_send.at[slot], pair_recv.at[slot], partner)
+
+    keep = pltpu.make_async_copy(own_ref, all_ref.at[me], local_sem)
+
+    @pl.when(chip < last)
+    def _():
+        to_right(own_ref, 0).start()
+
+    @pl.when(chip > 0)
+    def _():
+        to_left(own_ref, 0).start()
+
+    to_pair(own_ref, me).start()
+    keep.start()
+    for hop in range(1, chips):
+        @pl.when(chip >= hop)
+        def _():
+            owner = me - CORES * hop
+            block = all_ref.at[owner]
+            copy(block, owner, right_send.at[hop - 1], right_recv.at[hop - 1], right).wait_recv()
+
+            @pl.when(chip < last)
+            def _():
+                to_right(block, hop).start()
+
+            to_pair(block, owner).start()
+
+        @pl.when(chip + hop <= last)
+        def _():
+            owner = me + CORES * hop
+            block = all_ref.at[owner]
+            copy(block, owner, left_send.at[hop - 1], left_recv.at[hop - 1], left).wait_recv()
+
+            @pl.when(chip > 0)
+            def _():
+                to_left(block, hop).start()
+
+            to_pair(block, owner).start()
+
+    for hop in range(chips):
+        @pl.when((chip >= hop) & (chip < last))
+        def _():
+            to_right(own_ref, hop).wait_send()
+
+        @pl.when((chip + hop <= last) & (chip > 0))
+        def _():
+            to_left(own_ref, hop).wait_send()
+
+    for other in range(chips):
+        owner = other * CORES + core
+        to_pair(own_ref, owner).wait_send()
+        incoming = other * CORES + (1 - core)
+        copy(own_ref, incoming, pair_send.at[other], pair_recv.at[other], partner).wait_recv()
+    keep.wait()
+
+
+def line_gather(block):
+    owners = lax.axis_size("dom")
+    chips = owners // CORES
+    dma = pltpu.SemaphoreType.DMA((chips,))
+    return pl.pallas_call(
+        functools.partial(line_gather_kernel, chips),
+        out_shape=jax.ShapeDtypeStruct((owners,) + block.shape, block.dtype),
+        in_specs=[pl.BlockSpec(memory_space=pl.ANY)],
+        out_specs=pl.BlockSpec(memory_space=pl.ANY),
+        scratch_shapes=[dma] * 6 + [pltpu.SemaphoreType.DMA],
+        compiler_params=pltpu.CompilerParams(collective_id=0, has_side_effects=True),
+        name="line_gather",
+    )(block)
+
+
+def slot_kernel(which_ref, patch_ref, refs_ref, cols_ref, rows_ref, first_ref, second_ref, nyq_ref,
+                sums_ref, extra_ref):
+    slots, pixels = patch_ref.shape[0], patch_ref.shape[1]
+    half = pixels // 2
+    row_index = lax.broadcasted_iota(jnp.int32, (pixels, pixels), 0)
+    freq_y = jnp.where(row_index < half, row_index, row_index - pixels).astype(F32)
+
+    def pair(step, carry):
+        base = step * 2
+        both = jnp.concatenate([patch_ref[base], patch_ref[base + 1]], axis=1)
+        first = jnp.dot(first_ref[...], both, preferred_element_type=F32).astype(BF16)
+        for part in range(2):
+            slot = base + part
+            which = which_ref[slot]
+            mine = first[:, part * pixels : (part + 1) * pixels]
+            wide = jnp.concatenate([mine[:pixels], mine[pixels:]], axis=1)
+            spectrum = jnp.dot(wide, second_ref[...], preferred_element_type=F32)
+            line = lax.dot_general(
+                nyq_ref[...], mine, (((1,), (1,)), ((), ())), preferred_element_type=F32
+            )
+            turn = jnp.dot(cols_ref[slot], rows_ref[slot], preferred_element_type=F32)
+            ref = refs_ref[which, :pixels].astype(F32)
+            plain = spectrum[:, :pixels]
+            along = plain * ref
+            across = spectrum[:, pixels:] * ref
+            cosine = turn[:, :pixels]
+            sine = turn[:, pixels:]
+            real = cosine * along - sine * across
+            imag = sine * along + cosine * across
+            sums_ref[slot, 0:1] = jnp.sum(real, axis=0, keepdims=True)
+            sums_ref[slot, 1:2] = jnp.sum(imag, axis=0, keepdims=True)
+            sums_ref[slot, 2:3] = jnp.sum(imag * freq_y, axis=0, keepdims=True)
+            sums_ref[slot, 3:4] = jnp.sum(plain * plain, axis=0, keepdims=True)
+            sums_ref[slot, 4:5] = plain[half : half + 1]
+            sums_ref[slot, 5:6] = line[0:1, :pixels]
+            sums_ref[slot, 6:7] = line[0:1, pixels:]
+            sums_ref[slot, 7:8] = jnp.zeros((1, pixels), F32)
+            extra_ref[slot] = refs_ref[which, pixels:].astype(F32)
+        return carry
+
+    lax.fori_loop(0, slots // 2, pair, 0)
+
+
+def slot_sums(which, patches, refs, cols, rows, first, second, nyquist):
+    slots, pixels = patches.shape[0], patches.shape[1]
+    vmem = pl.BlockSpec(memory_space=pltpu.VMEM)
+    return pl.pallas_call(
+        slot_kernel,
+        out_shape=(
+            jax.ShapeDtypeStruct((slots, 8, pixels), F32),
+            jax.ShapeDtypeStruct((slots, EXTRA_ROWS, pixels), F32),
+        ),
+        in_specs=[pl.BlockSpec(memory_space=pltpu.SMEM)] + [vmem] * 7,
+        out_specs=(vmem, vmem),
+        compiler_params=pltpu.CompilerParams(vmem_limit_bytes=48 * 1024 * 1024),
+        name="slot_sums",
+    )(which, patches, refs, cols, rows, first, second, nyquist)
+
+
+def pass_tables(pixels):
+    half = pixels // 2
+    row_table, col_table = dft_tables(jnp.arange(pixels, dtype=jnp.int32), pixels)
+    cosine = col_table[:, :half]
+    sine = col_table[:, pixels : pixels + half]
+    real = jnp.concatenate([cosine, -sine], axis=0)
+    imag = jnp.concatenate([-sine, -cosine], axis=0)
+    second = jnp.concatenate([real, imag, imag, -real], axis=1)
+    nyquist = jnp.broadcast_to(col_table[:, half][None, :], (16, pixels))
+    return row_table, second, nyquist
+
+
+def slot_factors(focus, shifts, pixels):
+    half = pixels // 2
+    freq_y = signed_freq(jnp.arange(pixels, dtype=jnp.int32), pixels)
+    freq_x = jnp.arange(half, dtype=jnp.int32).astype(F32)
+    chi_y = math.pi * focus[:, None] * (freq_y * freq_y / (half * half))[None, :] + DELTA
+    chi_x = math.pi * focus[:, None] * (freq_x * freq_x / (half * half))[None, :]
+    step = 2.0 * math.pi / pixels
+    phi_y = step * shifts[:, 1:2] * freq_y[None, :]
+    phi_x = step * shifts[:, 0:1] * freq_x[None, :]
+    s_y, c_y, p_y, q_y = jnp.sin(chi_y), jnp.cos(chi_y), jnp.cos(phi_y), jnp.sin(phi_y)
+    c_x, s_x, p_x, q_x = jnp.cos(chi_x), jnp.sin(chi_x), jnp.cos(phi_x), jnp.sin(phi_x)
+    cols = jnp.stack([s_y * p_y, s_y * q_y, c_y * p_y, c_y * q_y], axis=2)
+    a, b, c, d = c_x * p_x, c_x * q_x, s_x * p_x, s_x * q_x
+    for_cos = jnp.stack([-a, b, -c, d], axis=1)
+    for_sin = jnp.stack([-b, -a, -d, -c], axis=1)
+    rows = jnp.concatenate([for_cos, for_cos, for_sin, for_sin], axis=2)
+    col_high, col_low = two_parts(cols)
+    row_high, row_low = two_parts(rows)
+    cols = jnp.concatenate([col_high, col_high, col_low, jnp.zeros_like(col_low)], axis=2)
+    rows = jnp.concatenate([row_high, row_low, row_high, jnp.zeros_like(row_low)], axis=1)
+    return cols, rows
+
+
+def line_terms(spec_re, spec_im, ref_re, ref_im, chi, phi):
+    contrast = -jnp.sin(chi + DELTA)
+    cosine = jnp.cos(phi)
+    sine = jnp.sin(phi)
+    model_re = contrast * (ref_re * cosine + ref_im * sine)
+    model_im = contrast * (ref_im * cosine - ref_re * sine)
+    return spec_re * model_re + spec_im * model_im, spec_im * model_re - spec_re * model_im
+
+
+def finish_terms(sums, extra, focus, shifts, pixels):
+    half = pixels // 2
+    k = jnp.arange(pixels, dtype=jnp.int32)
+    freq = signed_freq(k, pixels)
+    lane_freq = (k % half).astype(F32)
+    step = 2.0 * math.pi / pixels
+    norm = 1.0 / (half * half)
+    match = jnp.sum(sums[:, 0], axis=1)
+    grad_x = jnp.sum(sums[:, 1] * lane_freq, axis=1)
+    grad_y = jnp.sum(sums[:, 2], axis=1)
+    power = jnp.sum(sums[:, 3] * jnp.where(lane_freq > 0, 2.0, 1.0), axis=1)
+    d = focus[:, None]
+    s_x, s_y = shifts[:, 0:1], shifts[:, 1:2]
+    col_re, col_im = sums[:, 5], -sums[:, 6]
+    power = power + jnp.sum(col_re * col_re + col_im * col_im, axis=1)
+    along, across = line_terms(
+        col_re, col_im, extra[:, 0], extra[:, 1],
+        math.pi * d * (freq * freq * norm + 1.0), step * (freq * s_y - half * s_x),
+    )
+    match = match + jnp.sum(along, axis=1)
+    grad_x = grad_x - half * jnp.sum(across, axis=1)
+    grad_y = grad_y + jnp.sum(across * freq, axis=1)
+    f = lane_freq[:half]
+    along, across = line_terms(
+        sums[:, 4, :half], -sums[:, 4, half:], extra[:, 2, :half], extra[:, 2, half:],
+        math.pi * d * (f * f * norm + 1.0), step * (-f * s_x - half * s_y),
+    )
+    match = match + jnp.sum(along, axis=1)
+    grad_x = grad_x - jnp.sum(across * f, axis=1)
+    grad_y = grad_y - half * jnp.sum(across, axis=1)
+    place = jnp.where(
+        focus < 2.0, (focus - 1.0) * pixels, pixels + (focus - 2.0) * half
+    )
+    table_high = extra[:, 3:5].reshape(-1, 2 * pixels)
+    table_low = extra[:, 5:7].reshape(-1, 2 * pixels)
+    hit = place[:, None] == jnp.arange(2 * pixels, dtype=jnp.int32).astype(F32)[None, :]
+    model_power = jnp.sum(jnp.where(hit, table_high + table_low, 0.0), axis=1)
+    area = 1.0 / (pixels * pixels)
+    energy = (power + model_power - 2.0 * match) * area
+    return jnp.stack([energy, 2.0 * area * step * grad_x, 2.0 * area * step * grad_y], axis=0)
+
+
+def on_device_gathered(
+    patches, slot_view, slot_tilt, slot_pos, defocus, projections, warp_grid
+):
+    pixels = patches.shape[-1]
+    tilt_dev = warp_grid.shape[0]
+    node_count = warp_grid.shape[2]
+    tilt = slot_tilt[0]
+    refs = line_gather(fold_references(projections, pixels))
+    refs = refs.reshape(-1, pixels + EXTRA_ROWS, pixels)
+    weights = node_weights(slot_pos[0, 0].astype(F32), slot_pos[1, 0].astype(F32), GRID)
+    tilt_match = (tilt[:, None] == jnp.arange(tilt_dev, dtype=jnp.int32)[None, :]).astype(F32)
+    chosen = jnp.dot(
+        tilt_match, warp_grid.reshape(tilt_dev, -1), precision=lax.Precision.HIGHEST
+    ).reshape(-1, 2, node_count)
+    shifts = jnp.sum(chosen * weights[:, None, :], axis=2)
+    focus = defocus[0].astype(F32)
+    cols, rows = slot_factors(focus, shifts, pixels)
+    first, second, nyquist = pass_tables(pixels)
+    which = slot_view[0, :, 0] * tilt_dev + tilt
+    sums, extra = slot_sums(which, patches[0], refs, cols, rows, first, second, nyquist)
+    terms = finish_terms(sums, extra, focus, shifts, pixels)
+    coef = (tilt_match.T[:, None, :] * terms[None, 1:3, :]).reshape(2 * tilt_dev, -1)
+    gradient = jnp.dot(
+        coef, weights, precision=lax.Precision.HIGHEST, preferred_element_type=F32
+    ).reshape(tilt_dev, 2, node_count)
+    whole_grad = lax.psum(gradient, "dom")
+    new_warp = warp_grid - whole_grad / jnp.sqrt(
+        whole_grad * whole_grad + TRUST_FLOOR * TRUST_FLOOR
+    )
+    return (terms[:, None, :], new_warp)
+
+
 def solution(mesh):
+    body = on_device if mesh.shape["rep"] > 1 else on_device_gathered
     in_specs = (
         P(("groups", "tilt"), "dom", None, None),
         P(("groups", "tilt"), "dom", None),
@@ -194,5 +562,5 @@
     )
     out_specs = (P(None, ("groups", "tilt"), "dom"), P(("groups", "tilt"), None, None))
     return jax.shard_map(
-        on_device, mesh=mesh, in_specs=in_specs, out_specs=out_specs, check_vma=False
-    )
+        body, mesh=mesh, in_specs=in_specs, out_specs=out_specs, check_vma=False
+    )

time: 447 us -> 238 us (0.53)
  waiting for transfers between devices: 141 us -> 0 us
  Pallas kernels: 0 us -> 134 us
  other arithmetic: 149 us -> 34.6 us
  matrix products: 54.4 us -> 6.95 us
  local copies, waits for them, and re-layouts: 56.4 us -> 34.4 us
  starting transfers between devices: 14.9 us -> 0 us
    all_to_all x3 -> x0, waiting for transfers between devices: 141 us -> none  [the longest x1 136 us: on_device(): lax.all_to_all(patch_buffer, 'dom', split_axis=0, concat_axis=0, tiled=True)]
    pallas_call x0 -> x2, Pallas kernels: none -> 134 us  [the longest x1 101 us: line_gather(): pl.pallas_call(functools.partial(line_gather_kernel, chips), out_shape=ja...]
    reduce_sum x29 -> x9, other arithmetic: 136 us -> 14.4 us  [the longest x1 9.83 us: fold_references(): total = 0.5 * jnp.sum(power, axis=(1, 2))[:, None] - 0.5 * swing]
    gather x18 -> x0, local copies, waits for them, and re-layouts: 51.3 us -> none  [the longest x12 29.9 us: one_block(): ref_blk = projected_flat[index_blk]]
    dot_general x13 -> x6, matrix products: 54.4 us -> 6.95 us  [the longest x1 2.74 us: fold_references(): jnp.einsum('ncyx,cxl->nyl', refs, flip, preferred_element_type=F32)]
    all_to_all x3 -> x0, starting transfers between devices: 14.9 us -> none  [the longest x1 6.35 us: on_device(): lax.all_to_all(meta_buffer, 'dom', split_axis=0, concat_axis=0, tiled=True)]
    convert_element_type x2 -> x3, local copies, waits for them, and re-layouts: 0.81 us -> 11.6 us  [the longest x1 5 us: fold_references(): power.astype(BF16)]
    concatenate x0 -> x4, other arithmetic: none -> 10.4 us  [the longest x1 9.53 us: slot_factors(): jnp.concatenate([col_high, col_high, col_low, jnp.zeros_like(col_low)], a...]
  transfers between devices with their start and end apart: 3 -> 0, of which waited for: 2 -> 0; matrix products, arithmetic and copies ran while one was open for 6% -> 0% of each run, Pallas kernels for 0% -> 0%
where the time goes in v1:
time: 238 us
  Pallas kernels  134 us (56%)
  other arithmetic  34.6 us (15%)
  local copies, waits for them, and re-layouts  34.4 us (14%)
  blocking collectives  26.2 us (11%)
  matrix products  6.95 us (3%)
    pallas_call x1, Pallas kernels, line_gather(): pl.pallas_call(functools.partial(line_gather_kernel, chips), out_shape=ja...  101 us
    pallas_call x1, Pallas kernels, slot_sums(): pl.pallas_call(slot_kernel, out_shape=(jax.ShapeDtypeStruct((slots, 8, pi...  32.9 us
    psum x1, blocking collectives, on_device_gathered(): whole_grad = lax.psum(gradient, 'dom')  26.2 us
    reduce_sum x1, other arithmetic, fold_references(): total = 0.5 * jnp.sum(power, axis=(1, 2))[:, None] - 0.5 * swing  9.83 us
    concatenate x1, other arithmetic, slot_factors(): jnp.concatenate([col_high, col_high, col_low, jnp.zeros_like(col_low)], a...  9.53 us
    unnamed x13, local copies, waits for them, and re-layouts  9.46 us
    reshape x1, local copies, waits for them, and re-layouts, fold_references(): refs = projections.reshape(-1, 2, pixels, pixels)  7.53 us
    convert_element_type x1, local copies, waits for them, and re-layouts, fold_references(): power.astype(BF16)  5 us

profile of v1, /device:TPU:0, one launch (start us, length us, event | category | flops | bytes accessed | tf_op | source)
XLA Modules:
  0.0 237.6 jit_solution(4079664282366155972)
XLA Ops:
  0.6 0.7 multiply_bitcast_fusion.8
  1.4 0.1 subtract_maximum_fusion.1
  1.5 0.1 copy.86
  1.6 0.7 pad.50
  2.3 1.1 fusion.6
  3.4 0.7 fusion.81
  4.1 0.6 fusion.22
  4.7 3.3 %copy.87 = bf16[128,128,4]{2,1,0:T(8,128)(2,1)} copy(bf16[128,128,4]{1,0,2:T(8,128)(2,1)S(1)} %fusion.7) | data formatting | bytes 262144 | tf_op jit(solution)/shard_map/convert_element_type | solution.py:197
  8.0 3.3 %copy.89 = bf16[128,128,4]{2,1,0:T(8,128)(2,1)} copy(bf16[128,128,4]{1,0,2:T(8,128)(2,1)S(1)} %subtract_convert_fusion.1) | data formatting | bytes 262144 | tf_op jit(solution)/shard_map/convert_element_type | solution.py:198
  11.3 0.1 pad.41.clone
  11.4 9.5 %maximum_maximum_fusion.cols_ref = bf16[128,128,16]{2,1,0:T(8,128)(2,1)} fusion(bf16[128,128,4]{2,1,0:T(8,128)(2,1)} %copy.89, bf16[128,128,4]{2,1,0:T(8,128)(2,1)} %copy.87, bf16[16]{0:T(256)(128)(2,1)S(1)} %pad.41.clone), kind=kLoop, calls=%fused_computation.1 | loop fusion | flops 2097152 | bytes 786464 | tf_op jit(solution)/shard_map/concatenate | solution.py:464
  20.9 4.1 %fusion.90 = (f32[128,1,64]{2,1,0:T(1,128)S(1)}, f32[128,1,64]{2,1,0:T(1,128)S(1)}, f32[128,1,64]{2,1,0:T(1,128)S(1)}, f32[128,1,64]{2,1,0:T(1,128)S(1)}, f32[12...) fusion(f32[64]{0:T(128)S(1)} %iota_convert_fusion.1, f32[128]{0:T(128)S(1)} %get-tuple-element.58, ...), kind=kLoop, calls=%fused_computation.206 | loop fusion | flops 81920 | bytes 198144 | tf_op jit(solution)/shard_map/neg | solution.py:460
  25.1 1.9 subtract_convert_fusion
  27.0 0.7 maximum_maximum_fusion.1.rows_ref
  27.7 1.0 cosine_convert_fusion
  28.8 7.5 %copy.81 = bf16[4,10,2,128,128]{3,2,1,0,4:T(2,128)(2,1)} copy(bf16[4,10,2,128,128]{4,3,2,1,0:T(8,128)(2,1)} %param.12) | data formatting | bytes 5242880 | tf_op args[5]
  36.3 9.8 %fusion.95 = (f32[40]{0:T(128)S(1)}, bf16[40,1,128,128]{2,1,0,3:T(2,128)(2,1)}) fusion(bf16[40,2,128,128]{2,1,0,3:T(2,128)(2,1)} %bitcast.164), kind=kLoop, calls=%fused_computation.208 | loop fusion | flops 4587480 | bytes 3932320 | tf_op jit(solution)/shard_map/reduce_sum | solution.py:238
  46.1 5.0 %copy.84 = bf16[40,1,128,128]{3,2,0,1:T(8,128)(2,1)S(1)} copy(bf16[40,1,128,128]{2,1,0,3:T(2,128)(2,1)} %get-tuple-element.33) | data formatting | bytes 2621440 | tf_op jit(solution)/shard_map/convert_element_type | solution.py:233
  51.1 1.5 multiply_reduce_fusion
  52.6 0.1 subtract_convert_fusion.2
  52.7 7.5 %copy.82 = bf16[40,2,128,128]{3,2,1,0:T(8,128)(2,1)} copy(bf16[40,2,128,128]{2,1,0,3:T(2,128)(2,1)} %bitcast.165) | data formatting | bytes 5242880 | tf_op jit(solution)/shard_map/reshape | solution.py:203
  60.3 2.7 %fusion.4 = bf16[40,128,128]{2,1,0:T(8,128)(2,1)S(1)} fusion(bf16[40,2,128,128]{3,2,1,0:T(8,128)(2,1)} %copy.82, pred[128]{0:T(512)(128)(4,1)S(1)} %broadcast_compare_fusion, pred[128,128]{1,0:T(8,128)(4,1)S(1)} %iota_compare_fusion, pred[2,128]{1,0:T(4,128)(4,1)S(1)} %iota_compare_fusion.5), kind=kOutput, calls=%fused_computation.10 | convolution fusion | flops 336265216 | bytes 3948928 | tf_op jit(solution)/shard_map/ncyx,cxl->nyl/dot_general | solution.py:217
  63.1 0.8 fusion.16
  64.0 0.6 fusion.3
  64.6 0.7 slice_bitcast_fusion.5
  65.4 4.2 %concatenate.37.own_ref = bf16[40,136,128]{2,1,0:T(8,128)(2,1)} concatenate(bf16[40,128,128]{2,1,0:T(8,128)(2,1)S(1)} %fusion.3, bf16[40,2,128]{2,1,0:T(2,128)(2,1)S(1)} %slice_bitcast_fusion.5, bf16[40,1,128]{2,1,0:T(2,128)(2,1)S(1)} %slice.121, bf16[40,2,128]{2,1,0:T(2,128)(2,1)S(1)} %reshape.1370, bf16[40,2,128]{2,1,0:T(2,128)(2,1)S(1)} %reshape.1371, ...), dimensions={1} | concatenate | bytes 2785280 | tf_op jit(solution)/shard_map/concatenate | solution.py:251
  69.6 101.5 %line_gather.1 = bf16[8,40,136,128]{3,2,1,0:T(8,128)(2,1)} custom-call(bf16[40,136,128]{2,1,0:T(8,128)(2,1)} %concatenate.37.own_ref), custom_call_target="tpu_custom_call" | custom-call | tf_op jit(solution)/shard_map/line_gather/pallas_call | solution.py:364
  171.1 0.3 fusion.63
  171.4 0.1 pad_maximum_fusion.2.second_ref
  171.6 0.2 slice_reduce_fusion.2
  171.8 0.0 copy-done.2
  171.8 32.9 %slot_sums.1 = (f32[128,8,128]{2,1,0:T(8,128)S(1)}, f32[128,8,128]{2,1,0:T(8,128)S(1)}) custom-call(s32[128]{0:T(128)S(1)} %bitcast_add_fusion.2.which_ref, bf16[128,128,128]{2,1,0:T(8,128)(2,1)} %bitcast.167, bf16[320,136,128]{2,1,0:T(8,128)(2,1)} %bitcast.163, bf16[128,128,16]{2,1,0:T(8,128)(2,1)} %maximum_maximum_fusion.cols_ref, ...), custom_call_target="tpu_custom_call" | custom-call | tf_op jit(solution)/shard_map/slot_sums/pallas_call | solution.py:421
  204.7 0.0 copy-start.1
  204.7 0.1 copy.91
  204.8 0.1 copy.93
  205.0 0.6 fusion.34
  205.6 0.1 fusion.89
  205.7 0.2 slice.116
  206.0 0.6 add_reduce_fusion
  206.6 0.1 multiply_reduce_fusion.2
  206.7 1.1 slice_reduce_fusion.1
  207.8 0.1 multiply_reduce_fusion.3
  207.9 0.2 fusion.66
  208.2 26.2 %psum.7 = f32[10,2,256]{2,0,1:T(8,128)S(1)} all-reduce(f32[10,2,256]{2,0,1:T(8,128)S(1)} %fusion.66), channel_id=1, replica_groups=mesh['groups'=2,'dom'=8,'tilt'=2,'rep'=1] {'dom'}, use_global_device_ids=true, to_apply=%region_15.16 | all-reduce | flops 5120 | bytes 40960 | tf_op jit(solution)/shard_map/psum | solution.py:545
  234.4 0.6 copy.101
  235.0 0.1 multiply_reduce_fusion.4
  235.1 1.8 fusion.8
  237.0 0.6 copy.100
  (52 shorter events, 0.5 us)
Async XLA Ops:
  60.3 2.8 %copy-start = (bf16[40,2,128,128]{3,2,1,0:T(8,128)(2,1)S(1)}, bf16[40,2,128,128]{3,2,1,0:T(8,128)(2,1)}, u32[]{:S(2)}) copy-start(bf16[40,2,128,128]{3,2,1,0:T(8,128)(2,1)} %copy.82) | copy-start | bytes 7864324
  69.6 102.2 %copy-start.2 = (s32[1,128]{1,0:T(1,128)S(1)}, s32[1,128]{1,0:T(1,128)}, u32[]{:S(2)}) copy-start(s32[1,128]{1,0:T(1,128)} %param.9) | copy-start | bytes 1540
  69.6 102.2 %copy-start.3 = (s32[1,128,1]{1,2,0:T(1,128)S(1)}, s32[1,128,1]{1,2,0:T(1,128)}, u32[]{:S(2)}) copy-start(s32[1,128,1]{1,2,0:T(1,128)} %param.8) | copy-start | bytes 1540
  204.7 29.6 %copy-start.1 = (f32[10,2,256]{2,1,0:T(2,128)S(1)}, f32[10,2,256]{2,1,0:T(2,128)}, u32[]{:S(2)}) copy-start(f32[10,2,256]{2,1,0:T(2,128)} %param.13) | copy-start | bytes 61444

commit v2 on v0

--- a/solution.py
+++ b/solution.py
@@ -1,8 +1,11 @@
+import functools
 import math
 
 import jax
 import jax.numpy as jnp
 from jax import lax
+from jax.experimental import pallas as pl
+from jax.experimental.pallas import tpu as pltpu
 from jax.sharding import PartitionSpec as P
 
 GRID = 16
@@ -182,7 +185,499 @@
     return (slot_terms, new_warp)
 
 
+CORES = 2
+EXTRA_ROWS = 8
+DELTA = math.asin(AMPLITUDE)
+F32 = jnp.float32
+BF16 = jnp.bfloat16
+
+
+def fold_kernel(refs_ref, pick_ref, turn_ref, unit_ref, waves_ref, weights_ref, out_ref):
+    pixels = turn_ref.shape[0]
+    half = pixels // 2
+    lane = lax.broadcasted_iota(jnp.int32, (1, pixels), 1)
+    sign = jnp.where(lane < half, 1.0, -1.0)
+
+    def one(n, carry):
+        real, imag = refs_ref[n, 0], refs_ref[n, 1]
+        wide = jnp.concatenate([real, imag], axis=1)
+        picked = jnp.dot(wide, pick_ref[...], preferred_element_type=F32)
+        mirrored = picked[:, pixels:]
+        turned = jnp.dot(turn_ref[...], mirrored.astype(BF16), preferred_element_type=F32)
+        out_ref[n, :pixels] = (picked[:, :pixels] + sign * turned).astype(BF16)
+        tall = jnp.concatenate([real, imag], axis=0)
+        column = lax.dot_general(
+            unit_ref[...], tall, (((1,), (1,)), ((), ())), preferred_element_type=F32
+        )
+        r, i = real.astype(F32), imag.astype(F32)
+        power = r * r + i * i
+        mixed = jnp.dot(power.astype(BF16), waves_ref[...], preferred_element_type=F32)
+        swing = jnp.sum(mixed * weights_ref[...], axis=0, keepdims=True)
+        swing = swing[:, : 2 * pixels] + swing[:, 2 * pixels :]
+        total = 0.5 * jnp.sum(power) - 0.5 * swing
+        high = total.astype(BF16).astype(F32)
+        low = total - high
+        extra = jnp.concatenate(
+            [
+                column[0:1, :pixels],
+                column[0:1, pixels:],
+                mirrored[half : half + 1],
+                high[:, :pixels],
+                high[:, pixels:],
+                low[:, :pixels],
+                low[:, pixels:],
+                jnp.zeros((EXTRA_ROWS - 7, pixels), F32),
+            ],
+            axis=0,
+        )
+        out_ref[n, pixels:] = extra.astype(BF16)
+        return carry
+
+    lax.fori_loop(0, refs_ref.shape[0], one, 0)
+
+
+def fold_references(projections, pixels):
+    half = pixels // 2
+    refs = projections.reshape(-1, 2, pixels, pixels)
+    count = refs.shape[0]
+    k = jnp.arange(pixels, dtype=jnp.int32)
+    lane_freq = k % half
+    lane_part = k // half
+    chan = jnp.arange(2, dtype=jnp.int32)
+    same_part = chan[:, None, None] == lane_part[None, None, :]
+    pick = same_part & (k[None, :, None] == lane_freq[None, None, :])
+    flip = (
+        same_part
+        & (k[None, :, None] == pixels - lane_freq[None, None, :])
+        & (lane_freq > 0)[None, None, :]
+    )
+    picks = jnp.concatenate([pick, flip], axis=2).reshape(2 * pixels, 2 * pixels).astype(BF16)
+    turn = (((k[:, None] + k[None, :]) % pixels == 0) & (k != half)[:, None]).astype(BF16)
+    unit = jnp.broadcast_to((k == half).astype(BF16)[None, :], (16, pixels))
+    table = jnp.arange(2 * pixels, dtype=jnp.int32)
+    focus = jnp.where(
+        table < pixels, 1.0 + table / pixels, 2.0 + (table - pixels) / (pixels // 2)
+    ).astype(F32)
+    freq = signed_freq(k, pixels)
+    chi = math.pi * focus[None, :] * (freq * freq / (half * half))[:, None]
+    chi = jnp.concatenate([chi, chi + 0.25 * math.pi], axis=1) * 2.0
+    waves = jnp.cos(jnp.concatenate([chi[:, : 2 * pixels], chi[:, 2 * pixels :] - math.pi], axis=1))
+    weights = jnp.cos(chi + 2.0 * DELTA)
+    rows = pixels + EXTRA_ROWS
+    group = math.gcd(count, 5)
+    full = lambda x: pl.BlockSpec(x.shape, lambda i: (0, 0))
+    tables = (picks, turn, unit, waves.astype(BF16), weights)
+    return pl.pallas_call(
+        fold_kernel,
+        grid=(count // group,),
+        out_shape=jax.ShapeDtypeStruct((count, rows, pixels), BF16),
+        in_specs=[pl.BlockSpec((group, 2, pixels, pixels), lambda i: (i, 0, 0, 0))]
+        + [full(x) for x in tables],
+        out_specs=pl.BlockSpec((group, rows, pixels), lambda i: (i, 0, 0)),
+        name="fold_references",
+    )(refs, *tables)
+
+
+def gather_kernel(chips, cap, src_ref, which_ref, own_ref, patch_ref, meta_ref, first_ref,
+                  second_ref, nyq_ref, sums_ref, extra_ref, factor_ref, *rest):
+    lefts, rights = rest[: chips - 1], rest[chips - 1 : 2 * chips - 2]
+    left_pairs, right_pairs = rest[2 * chips - 2 : 3 * chips - 3], rest[3 * chips - 3 : 4 * chips - 4]
+    (pair_ref, rs, rr, ls, lr, lps, lpr, rps, rpr, ps, pr) = rest[4 * chips - 4 :]
+    pixels = patch_ref.shape[1]
+    half = pixels // 2
+    me = lax.axis_index("dom")
+    chip = me // CORES
+    core = me % CORES
+    partner = chip * CORES + (1 - core)
+    right = me + CORES
+    left = me - CORES
+    last = chips - 1
+    barrier = pltpu.get_barrier_semaphore()
+
+    def greet(device):
+        pl.semaphore_signal(
+            barrier, inc=1, device_id={"dom": device}, device_id_type=pl.DeviceIdType.MESH
+        )
+
+    greet(partner)
+
+    @pl.when(chip < last)
+    def _():
+        greet(right)
+
+    @pl.when(chip > 0)
+    def _():
+        greet(left)
+
+    inner = (chip > 0) & (chip < last)
+
+    @pl.when(inner)
+    def _():
+        pl.semaphore_wait(barrier, 3)
+
+    @pl.when(jnp.logical_not(inner))
+    def _():
+        pl.semaphore_wait(barrier, 2)
+
+    def copy(src, dst, send, recv, target):
+        return pltpu.make_async_remote_copy(
+            src_ref=src, dst_ref=dst, send_sem=send, recv_sem=recv,
+            device_id={"dom": target}, device_id_type=pl.DeviceIdType.MESH,
+        )
+
+    def to_right(hop):
+        src = own_ref if hop == 0 else lefts[hop - 1]
+        return copy(src, lefts[hop], rs.at[hop], rr.at[hop], right)
+
+    def to_left(hop):
+        src = own_ref if hop == 0 else rights[hop - 1]
+        return copy(src, rights[hop], ls.at[hop], lr.at[hop], left)
+
+    def pair_left(hop):
+        return copy(lefts[hop], left_pairs[hop], lps.at[hop], lpr.at[hop], partner)
+
+    def pair_right(hop):
+        return copy(rights[hop], right_pairs[hop], rps.at[hop], rpr.at[hop], partner)
+
+    pair_own = copy(own_ref, pair_ref, ps, pr, partner)
+
+    @pl.when(chip < last)
+    def _():
+        to_right(0).start()
+
+    @pl.when(chip > 0)
+    def _():
+        to_left(0).start()
+
+    pair_own.start()
+
+    row_index = lax.broadcasted_iota(jnp.int32, (pixels, pixels), 0)
+    freq_y = jnp.where(row_index < half, row_index, row_index - pixels).astype(F32)
+    lane = lax.broadcasted_iota(jnp.int32, (cap, pixels), 1)
+    line_y = jnp.where(lane < half, lane, lane - pixels).astype(F32)
+    line_x = jnp.where(lane < half, lane, lane - half).astype(F32)
+    norm = 1.0 / (half * half)
+    step_angle = 2.0 * math.pi / pixels
+
+    def factors(block, carry):
+        rows = pl.ds(pl.multiple_of(block * cap, 8), cap)
+        focus, shift_x, shift_y = meta_ref[0, rows], meta_ref[1, rows], meta_ref[2, rows]
+        chi_y = math.pi * focus * (line_y * line_y * norm) + DELTA
+        chi_x = math.pi * focus * (line_x * line_x * norm)
+        phi_y = step_angle * shift_y * line_y
+        phi_x = step_angle * shift_x * line_x
+        s_y, c_y, p_y, q_y = jnp.sin(chi_y), jnp.cos(chi_y), jnp.cos(phi_y), jnp.sin(phi_y)
+        c_x, s_x, p_x, q_x = jnp.cos(chi_x), jnp.sin(chi_x), jnp.cos(phi_x), jnp.sin(phi_x)
+        values = (s_y * p_y, s_y * q_y, c_y * p_y, c_y * q_y,
+                  c_x * p_x, c_x * q_x, s_x * p_x, s_x * q_x)
+        for place, value in enumerate(values):
+            factor_ref[rows, place] = value
+        return carry
+
+    lax.fori_loop(0, meta_ref.shape[1] // cap, factors, 0)
+
+    def process(refs_ref, owner):
+        def pair(step, carry):
+            base = owner * cap + step * 2
+            both = jnp.concatenate(
+                [patch_ref[src_ref[base]], patch_ref[src_ref[base + 1]]], axis=1
+            )
+            first = jnp.dot(first_ref[...], both, preferred_element_type=F32).astype(BF16)
+            for part in range(2):
+                slot = base + part
+                which = which_ref[slot]
+                mine = first[:, part * pixels : (part + 1) * pixels]
+                wide = jnp.concatenate([mine[:pixels], mine[pixels:]], axis=1)
+                spectrum = jnp.dot(wide, second_ref[...], preferred_element_type=F32)
+                line = lax.dot_general(
+                    nyq_ref[...], mine, (((1,), (1,)), ((), ())), preferred_element_type=F32
+                )
+                factor = factor_ref[slot]
+                a, b, c, d = factor[4:5], factor[5:6], factor[6:7], factor[7:8]
+                cols = factor[0:4]
+                rows = jnp.concatenate(
+                    [
+                        jnp.concatenate([-a, b, -c, d], axis=0),
+                        jnp.concatenate([-b, -a, -d, -c], axis=0),
+                    ],
+                    axis=1,
+                )
+                col_high = cols.astype(BF16).astype(F32)
+                row_high = rows.astype(BF16).astype(F32)
+                col_low, row_low = cols - col_high, rows - row_high
+                col_all = jnp.concatenate(
+                    [col_high, col_high, col_low, jnp.zeros_like(col_low)], axis=0
+                ).astype(BF16)
+                row_all = jnp.concatenate(
+                    [row_high, row_low, row_high, jnp.zeros_like(row_low)], axis=0
+                ).astype(BF16)
+                turn = lax.dot_general(
+                    col_all, row_all, (((0,), (0,)), ((), ())), preferred_element_type=F32
+                )
+                ref = refs_ref[which, :pixels].astype(F32)
+                plain = spectrum[:, :pixels]
+                along = plain * ref
+                across = spectrum[:, pixels:] * ref
+                cosine = turn[:, :pixels]
+                sine = turn[:, pixels:]
+                real = cosine * along - sine * across
+                imag = sine * along + cosine * across
+                sums_ref[slot] = jnp.concatenate(
+                    [
+                        jnp.sum(real, axis=0, keepdims=True),
+                        jnp.sum(imag, axis=0, keepdims=True),
+                        jnp.sum(imag * freq_y, axis=0, keepdims=True),
+                        jnp.sum(plain * plain, axis=0, keepdims=True),
+                        plain[half : half + 1],
+                        line[0:1, :pixels],
+                        line[0:1, pixels:],
+                        jnp.zeros((1, pixels), F32),
+                    ],
+                    axis=0,
+                )
+                extra_ref[slot] = refs_ref[which, pixels:].astype(F32)
+            return carry
+
+        lax.fori_loop(0, cap // 2, pair, 0)
+
+    process(own_ref, me)
+    pair_own.wait_recv()
+    process(pair_ref, partner)
+    for hop in range(1, chips):
+        @pl.when(chip >= hop)
+        def _():
+            to_right(hop - 1).wait_recv()
+            if hop < last:
+                @pl.when(chip < last)
+                def _():
+                    to_right(hop).start()
+            pair_left(hop - 1).start()
+
+        @pl.when(chip + hop <= last)
+        def _():
+            to_left(hop - 1).wait_recv()
+            if hop < last:
+                @pl.when(chip > 0)
+                def _():
+                    to_left(hop).start()
+            pair_right(hop - 1).start()
+
+        @pl.when(chip >= hop)
+        def _():
+            process(lefts[hop - 1], me - CORES * hop)
+            pair_left(hop - 1).wait_recv()
+            process(left_pairs[hop - 1], partner - CORES * hop)
+
+        @pl.when(chip + hop <= last)
+        def _():
+            process(rights[hop - 1], me + CORES * hop)
+            pair_right(hop - 1).wait_recv()
+            process(right_pairs[hop - 1], partner + CORES * hop)
+
+    pair_own.wait_send()
+    for hop in range(last):
+        @pl.when((chip >= hop) & (chip < last))
+        def _():
+            to_right(hop).wait_send()
+
+        @pl.when((chip + hop <= last) & (chip > 0))
+        def _():
+            to_left(hop).wait_send()
+
+        @pl.when(chip >= hop + 1)
+        def _():
+            pair_left(hop).wait_send()
+
+        @pl.when(chip + hop + 1 <= last)
+        def _():
+            pair_right(hop).wait_send()
+
+
+def gather_sums(cap, src, which, own, patches, meta, first, second, nyquist):
+    chips = lax.axis_size("dom") // CORES
+    pixels = patches.shape[1]
+    padded = src.shape[0]
+    vmem = pl.BlockSpec(memory_space=pltpu.VMEM)
+    smem = pl.BlockSpec(memory_space=pltpu.SMEM)
+    dma = pltpu.SemaphoreType.DMA((chips,))
+    return pl.pallas_call(
+        functools.partial(gather_kernel, chips, cap),
+        out_shape=(
+            jax.ShapeDtypeStruct((padded, 8, pixels), F32),
+            jax.ShapeDtypeStruct((padded, EXTRA_ROWS, pixels), F32),
+        ),
+        in_specs=[smem, smem] + [vmem] * 6,
+        out_specs=(vmem, vmem),
+        scratch_shapes=[pltpu.VMEM((padded, 8, pixels), F32)]
+        + [pltpu.VMEM(own.shape, own.dtype)] * (4 * (chips - 1) + 1)
+        + [dma] * 8
+        + [pltpu.SemaphoreType.DMA] * 2,
+        compiler_params=pltpu.CompilerParams(
+            collective_id=0, has_side_effects=True, vmem_limit_bytes=56 * 1024 * 1024
+        ),
+        name="gather_sums",
+    )(src, which, own, patches, meta, first, second, nyquist)
+
+
+def step_kernel(owners, grad_ref, warp_ref, out_ref, held_ref, send_sem, recv_sem):
+    me = lax.axis_index("dom")
+    barrier = pltpu.get_barrier_semaphore()
+    for hop in range(1, owners):
+        pl.semaphore_signal(
+            barrier, inc=1, device_id={"dom": lax.rem(me + hop, owners)},
+            device_id_type=pl.DeviceIdType.MESH,
+        )
+    pl.semaphore_wait(barrier, owners - 1)
+
+    def copy(hop):
+        return pltpu.make_async_remote_copy(
+            src_ref=grad_ref, dst_ref=held_ref.at[hop - 1], send_sem=send_sem.at[hop - 1],
+            recv_sem=recv_sem.at[hop - 1], device_id={"dom": lax.rem(me + hop, owners)},
+            device_id_type=pl.DeviceIdType.MESH,
+        )
+
+    for hop in range(1, owners):
+        copy(hop).start()
+    for hop in range(1, owners):
+        copy(hop).wait()
+    total = grad_ref[...]
+    for hop in range(1, owners):
+        total = total + held_ref[hop - 1]
+    out_ref[...] = warp_ref[...] - total / jnp.sqrt(total * total + TRUST_FLOOR * TRUST_FLOOR)
+
+
+def warp_step(gradient, warp):
+    owners = lax.axis_size("dom")
+    vmem = pl.BlockSpec(memory_space=pltpu.VMEM)
+    dma = pltpu.SemaphoreType.DMA((owners - 1,))
+    return pl.pallas_call(
+        functools.partial(step_kernel, owners),
+        out_shape=jax.ShapeDtypeStruct(warp.shape, F32),
+        in_specs=[vmem, vmem],
+        out_specs=vmem,
+        scratch_shapes=[pltpu.VMEM((owners - 1,) + warp.shape, F32), dma, dma],
+        compiler_params=pltpu.CompilerParams(collective_id=1, has_side_effects=True),
+        name="warp_step",
+    )(gradient, warp)
+
+
+def pass_tables(pixels):
+    half = pixels // 2
+    row_table, col_table = dft_tables(jnp.arange(pixels, dtype=jnp.int32), pixels)
+    cosine = col_table[:, :half]
+    sine = col_table[:, pixels : pixels + half]
+    real = jnp.concatenate([cosine, -sine], axis=0)
+    imag = jnp.concatenate([-sine, -cosine], axis=0)
+    second = jnp.concatenate([real, imag, imag, -real], axis=1)
+    nyquist = jnp.broadcast_to(col_table[:, half][None, :], (16, pixels))
+    return row_table, second, nyquist
+
+
+def line_terms(spec_re, spec_im, ref_re, ref_im, chi, phi):
+    contrast = -jnp.sin(chi + DELTA)
+    cosine = jnp.cos(phi)
+    sine = jnp.sin(phi)
+    model_re = contrast * (ref_re * cosine + ref_im * sine)
+    model_im = contrast * (ref_im * cosine - ref_re * sine)
+    return spec_re * model_re + spec_im * model_im, spec_im * model_re - spec_re * model_im
+
+
+def finish_terms(sums, extra, focus, shifts, pixels):
+    half = pixels // 2
+    k = jnp.arange(pixels, dtype=jnp.int32)
+    freq = signed_freq(k, pixels)
+    lane_freq = (k % half).astype(F32)
+    step = 2.0 * math.pi / pixels
+    norm = 1.0 / (half * half)
+    match = jnp.sum(sums[:, 0], axis=1)
+    grad_x = jnp.sum(sums[:, 1] * lane_freq, axis=1)
+    grad_y = jnp.sum(sums[:, 2], axis=1)
+    power = jnp.sum(sums[:, 3] * jnp.where(lane_freq > 0, 2.0, 1.0), axis=1)
+    d = focus[:, None]
+    s_x, s_y = shifts[:, 0:1], shifts[:, 1:2]
+    col_re, col_im = sums[:, 5], -sums[:, 6]
+    power = power + jnp.sum(col_re * col_re + col_im * col_im, axis=1)
+    along, across = line_terms(
+        col_re, col_im, extra[:, 0], extra[:, 1],
+        math.pi * d * (freq * freq * norm + 1.0), step * (freq * s_y - half * s_x),
+    )
+    match = match + jnp.sum(along, axis=1)
+    grad_x = grad_x - half * jnp.sum(across, axis=1)
+    grad_y = grad_y + jnp.sum(across * freq, axis=1)
+    f = lane_freq[:half]
+    along, across = line_terms(
+        sums[:, 4, :half], -sums[:, 4, half:], extra[:, 2, :half], extra[:, 2, half:],
+        math.pi * d * (f * f * norm + 1.0), step * (-f * s_x - half * s_y),
+    )
+    match = match + jnp.sum(along, axis=1)
+    grad_x = grad_x - jnp.sum(across * f, axis=1)
+    grad_y = grad_y - half * jnp.sum(across, axis=1)
+    place = jnp.where(
+        focus < 2.0, (focus - 1.0) * pixels, pixels + (focus - 2.0) * half
+    )
+    table_high = extra[:, 3:5].reshape(-1, 2 * pixels)
+    table_low = extra[:, 5:7].reshape(-1, 2 * pixels)
+    hit = place[:, None] == jnp.arange(2 * pixels, dtype=jnp.int32).astype(F32)[None, :]
+    model_power = jnp.sum(jnp.where(hit, table_high + table_low, 0.0), axis=1)
+    area = 1.0 / (pixels * pixels)
+    energy = (power + model_power - 2.0 * match) * area
+    return jnp.stack([energy, 2.0 * area * step * grad_x, 2.0 * area * step * grad_y], axis=0)
+
+
+def on_device_gathered(
+    patches, slot_view, slot_tilt, slot_pos, defocus, projections, warp_grid
+):
+    owners = lax.axis_size("dom")
+    pixels = patches.shape[-1]
+    slots = patches.shape[1]
+    view_dev = projections.shape[0]
+    tilt_dev = warp_grid.shape[0]
+    node_count = warp_grid.shape[2]
+    cap = 3 * slots // (2 * owners)
+    padded = owners * cap
+    exact = functools.partial(
+        jnp.dot, precision=lax.Precision.HIGHEST, preferred_element_type=F32
+    )
+    own = fold_references(projections, pixels)
+    tilt = slot_tilt[0]
+    view = slot_view[0, :, 0]
+    slot_iota = jnp.arange(slots, dtype=jnp.int32)
+    owner_of = view // view_dev
+    ahead = (owner_of[:, None] == owner_of[None, :]) & (slot_iota[None, :] < slot_iota[:, None])
+    target = owner_of * cap + jnp.sum(ahead.astype(jnp.int32), axis=1)
+    matches = (target[None, :] == jnp.arange(padded, dtype=jnp.int32)[:, None]).astype(F32)
+    weights = node_weights(slot_pos[0, 0].astype(F32), slot_pos[1, 0].astype(F32), GRID)
+    tilt_match = (tilt[:, None] == jnp.arange(tilt_dev, dtype=jnp.int32)[None, :]).astype(F32)
+    chosen = exact(tilt_match, warp_grid.reshape(tilt_dev, -1))
+    shift_x = jnp.sum(chosen[:, :node_count] * weights, axis=1)
+    shift_y = jnp.sum(chosen[:, node_count:] * weights, axis=1)
+    facts = jnp.stack(
+        [
+            slot_iota.astype(F32),
+            ((view % view_dev) * tilt_dev + tilt).astype(F32),
+            defocus[0].astype(F32),
+            shift_x,
+            shift_y,
+        ],
+        axis=1,
+    )
+    facts = exact(matches, facts)
+    src = jnp.round(facts[:, 0]).astype(jnp.int32)
+    which = jnp.round(facts[:, 1]).astype(jnp.int32)
+    focus = facts[:, 2]
+    shifts = facts[:, 3:5]
+    meta = jnp.broadcast_to(facts[:, 2:5].T[:, :, None], (3, padded, pixels))
+    first, second, nyquist = pass_tables(pixels)
+    sums, extra = gather_sums(cap, src, which, own, patches[0], meta, first, second, nyquist)
+    terms = exact(finish_terms(sums, extra, focus, shifts, pixels), matches)
+    coef = (tilt_match.T[:, None, :] * terms[None, 1:3, :]).reshape(2 * tilt_dev, -1)
+    gradient = exact(coef, weights).reshape(tilt_dev, 2 * node_count)
+    new_warp = warp_step(gradient, warp_grid.reshape(tilt_dev, 2 * node_count))
+    return (terms[:, None, :], new_warp.reshape(warp_grid.shape))
+
+
 def solution(mesh):
+    body = on_device if mesh.shape["rep"] > 1 else on_device_gathered
     in_specs = (
         P(("groups", "tilt"), "dom", None, None),
         P(("groups", "tilt"), "dom", None),
@@ -194,5 +689,5 @@
     )
     out_specs = (P(None, ("groups", "tilt"), "dom"), P(("groups", "tilt"), None, None))
     return jax.shard_map(
-        on_device, mesh=mesh, in_specs=in_specs, out_specs=out_specs, check_vma=False
-    )
+        body, mesh=mesh, in_specs=in_specs, out_specs=out_specs, check_vma=False
+    )

time: 447 us -> 169 us (0.38)
  waiting for transfers between devices: 141 us -> 0 us
  Pallas kernels: 0 us -> 139 us
  other arithmetic: 149 us -> 16.4 us
  matrix products: 54.4 us -> 1.46 us
  local copies, waits for them, and re-layouts: 56.4 us -> 9.9 us
  blocking collectives: 26.7 us -> 0 us
  starting transfers between devices: 14.9 us -> 0 us
    all_to_all x3 -> x0, waiting for transfers between devices: 141 us -> none  [the longest x1 136 us: on_device(): lax.all_to_all(patch_buffer, 'dom', split_axis=0, concat_axis=0, tiled=True)]
    pallas_call x0 -> x3, Pallas kernels: none -> 139 us  [the longest x1 112 us: gather_sums(): pl.pallas_call(functools.partial(gather_kernel, chips, cap), out_shape=(j...]
    reduce_sum x29 -> x10, other arithmetic: 136 us -> 5.71 us  [the longest x1 1.97 us: finish_terms(): model_power = jnp.sum(jnp.where(hit, table_high + table_low, 0.0), axis=1)]
    dot_general x13 -> x4, matrix products: 54.4 us -> 1.46 us  [the longest x1 0.97 us: on_device_gathered(): chosen = exact(tilt_match, warp_grid.reshape(tilt_dev, -1))]
    gather x18 -> x0, local copies, waits for them, and re-layouts: 51.3 us -> none  [the longest x12 29.9 us: one_block(): ref_blk = projected_flat[index_blk]]
    psum x1 -> x0, blocking collectives: 26.7 us -> none  [on_device(): whole_grad = lax.psum(gradient, ('dom', 'rep'))]
    all_to_all x3 -> x0, starting transfers between devices: 14.9 us -> none  [the longest x1 6.35 us: on_device(): lax.all_to_all(meta_buffer, 'dom', split_axis=0, concat_axis=0, tiled=True)]
    select_n x17 -> x5, other arithmetic: 7.38 us -> 1.37 us  [the longest x1 0.69 us: finish_terms(): jnp.where(focus < 2.0, (focus - 1.0) * pixels, pixels + (focus - 2.0) * h...]
  transfers between devices with their start and end apart: 3 -> 0, of which waited for: 2 -> 0; matrix products, arithmetic and copies ran while one was open for 6% -> 0% of each run, Pallas kernels for 0% -> 0%
where the time goes in v2:
time: 169 us; the launch traced here: 168 us
  Pallas kernels  139 us (82%)
  other arithmetic  16.4 us (10%)
  local copies, waits for them, and re-layouts  9.9 us (6%)
    pallas_call x1, Pallas kernels, gather_sums(): pl.pallas_call(functools.partial(gather_kernel, chips, cap), out_shape=(j...  112 us
    pallas_call x1, Pallas kernels, fold_references(): pl.pallas_call(fold_kernel, grid=(count // group,), out_shape=jax.ShapeDt...  18.2 us
    pallas_call x1, Pallas kernels, warp_step(): pl.pallas_call(functools.partial(step_kernel, owners), out_shape=jax.Shap...  9.27 us

profile of v2, /device:TPU:0, one launch (start us, length us, event | category | flops | bytes accessed | tf_op | source)
XLA Modules:
  0.0 167.8 jit_solution(14201509699154967949)
XLA Ops:
  0.6 0.3 fusion.34
  1.0 0.8 pad_maximum_fusion.second_ref
  1.8 0.7 multiply_bitcast_fusion.1
  2.5 0.1 subtract_maximum_fusion.1
  2.6 0.1 copy.25
  2.7 0.7 pad.22
  3.4 0.0 copy-start.2
  3.5 1.0 fusion.31
  4.4 0.1 fusion.2
  4.5 0.7 iota_convert_fusion.2
  5.2 0.7 bitcast_convert_fusion
  5.9 0.7 and_select_fusion.3
  6.6 0.2 convert_reduce_fusion
  6.8 0.7 multiply_add_fusion.1
  7.4 0.1 fusion.16
  7.6 0.7 compare_select_fusion.1
  8.3 0.9 broadcast_in_dim.20.meta_ref
  9.2 0.1 broadcast_multiply_fusion
  9.3 1.6 add_cosine_fusion
  10.9 1.5 fusion.waves_ref
  12.5 0.7 add_convert_fusion.pick_ref
  13.2 0.7 fusion.29.turn_ref
  13.9 0.6 broadcast_in_dim.19.unit_ref
  14.5 18.2 %fold_references.1.own_ref = bf16[40,136,128]{2,1,0:T(8,128)(2,1)} custom-call(bf16[40,2,128,128]{3,2,1,0:T(8,128)(2,1)} %bitcast.121, bf16[256,256]{1,0:T(8,128)(2,1)} %add_convert_fusion.pick_ref, bf16[128,128]{1,0:T(8,128)(2,1)} %fusion.29.turn_ref, bf16[16,128]{1,0:T(8,128)(2,1)} %broadcast_in_dim.19.unit_ref, bf16[128,512]{1,0:T(8,128)(2,1)} %fusion.waves_ref, ...), custom_call_target="tpu_custom_call" | custom-call | tf_op jit(solution)/shard_map/fold_references/pallas_call | solution.py:270
  32.7 0.2 slice_reduce_fusion.2
  32.9 0.6 broadcast_in_dim.22.nyq_ref
  33.5 0.6 fusion.4.first_ref
  34.1 111.6 %gather_sums.1 = (f32[192,8,128]{2,1,0:T(8,128)}, f32[192,8,128]{2,1,0:T(8,128)}) custom-call(s32[192]{0:T(256)} %bitcast.143, s32[192]{0:T(256)} %bitcast.142, bf16[40,136,128]{2,1,0:T(8,128)(2,1)} %fold_references.1.own_ref, bf16[128,128,128]{2,1,0:T(8,128)(2,1)} %bitcast.120, f32[3,192,128]{2,1,0:T(8,128)} %broadcast_in_dim.20.meta_ref, ...), custom_call_target="tpu_custom_call" | custom-call | tf_op jit(solution)/shard_map/gather_sums/pallas_call | solution.py:503
  145.8 1.4 copy.29
  147.2 0.0 copy-start.3
  147.2 1.2 slice.122
  148.4 1.3 copy.27
  149.7 0.9 fusion.10
  150.6 0.3 slice.126
  150.9 0.9 add_reduce_fusion
  151.8 2.0 %fusion.1 = f32[192]{0:T(256)S(1)} fusion(f32[192,8,128]{2,1,0:T(8,128)S(1)} %copy-done, f32[2,128]{1,0:T(2,128)S(1)} %add_convert_fusion.1, f32[192]{0:T(256)S(1)} %bitcast.137), kind=kLoop, calls=%fused_computation.6 | loop fusion | flops 196416 | bytes 395776 | tf_op jit(solution)/shard_map/reduce_sum | solution.py:621
  153.8 1.1 slice_reduce_fusion.1
  155.0 0.1 multiply_reduce_fusion.3
  155.1 0.1 fusion.59
  155.3 0.2 multiply_reduce_fusion.1
  155.4 0.1 multiply_reduce_fusion.2
  155.6 0.1 fusion.15
  155.7 0.0 copy-done.3
  155.8 0.2 fusion.62
  156.0 0.6 reshape.613.grad_ref
  156.6 9.3 %warp_step.1 = f32[10,512]{1,0:T(8,128)} custom-call(f32[10,512]{1,0:T(8,128)} %reshape.613.grad_ref, f32[10,512]{1,0:T(8,128)} %bitcast.129), custom_call_target="tpu_custom_call" | custom-call | tf_op jit(solution)/shard_map/warp_step/pallas_call | solution.py:553
  165.9 1.4 reshape.614
  167.3 0.6 copy.33
  (39 shorter events, 0.4 us)
Async XLA Ops:
  3.4 29.2 %copy-start.2 = (f32[2,8,2,256]{3,1,2,0:T(8,128)}, f32[2,8,2,256]{3,1,2,0:T(8,128)S(1)}, u32[]{:S(2)}) copy-start(f32[2,8,2,256]{3,1,2,0:T(8,128)S(1)} %copy.34) | copy-start | bytes 98308
  145.7 4.9 %copy-start = (f32[192,8,128]{2,1,0:T(8,128)S(1)}, f32[192,8,128]{2,1,0:T(8,128)}, u32[]{:S(2)}) copy-start(f32[192,8,128]{2,1,0:T(8,128)} %get-tuple-element.5) | copy-start | bytes 2359300
  145.8 8.1 %copy-start.1 = (f32[192,8,128]{2,1,0:T(8,128)S(1)}, f32[192,8,128]{2,1,0:T(8,128)}, u32[]{:S(2)}) copy-start(f32[192,8,128]{2,1,0:T(8,128)} %get-tuple-element.4) | copy-start | bytes 2359300
  147.2 8.5 %copy-start.3 = (s32[1,128]{1,0:T(1,128)S(1)}, s32[1,128]{1,0:T(1,128)}, u32[]{:S(2)}) copy-start(s32[1,128]{1,0:T(1,128)} %param.9) | copy-start | bytes 1540

commit v3 on v2

--- a/solution.py
+++ b/solution.py
@@ -233,7 +233,7 @@
         out_ref[n, pixels:] = extra.astype(BF16)
         return carry
 
-    lax.fori_loop(0, refs_ref.shape[0], one, 0)
+    lax.fori_loop(0, refs_ref.shape[0], one, 0, unroll=True)
 
 
 def fold_references(projections, pixels):

time: 169 us -> 161 us (0.953)
  Pallas kernels: 139 us -> 132 us
    pallas_call x1, Pallas kernels: 18.2 us -> 10.7 us  [fold_references(): pl.pallas_call(fold_kernel, grid=(count // group,), out_shape=jax.ShapeDt...]
where the time goes in v3:
time: 161 us; the launch traced here: 160 us
  Pallas kernels  132 us (82%)
  other arithmetic  16.4 us (10%)
  local copies, waits for them, and re-layouts  9.9 us (6%)
    pallas_call x1, Pallas kernels, gather_sums(): pl.pallas_call(functools.partial(gather_kernel, chips, cap), out_shape=(j...  112 us
    pallas_call x1, Pallas kernels, fold_references(): pl.pallas_call(fold_kernel, grid=(count // group,), out_shape=jax.ShapeDt...  10.7 us
    pallas_call x1, Pallas kernels, warp_step(): pl.pallas_call(functools.partial(step_kernel, owners), out_shape=jax.Shap...  9.27 us

profile of v3, /device:TPU:0, one launch (start us, length us, event | category | flops | bytes accessed | tf_op | source)
XLA Modules:
  0.0 160.3 jit_solution(6628258861343450916)
XLA Ops:
  0.6 0.3 fusion.34
  1.0 0.8 pad_maximum_fusion.second_ref
  1.8 0.7 multiply_bitcast_fusion.1
  2.5 0.1 subtract_maximum_fusion.1
  2.6 0.1 copy.25
  2.7 0.7 pad.22
  3.4 0.0 copy-start.2
  3.5 1.0 fusion.31
  4.4 0.1 fusion.2
  4.5 0.7 iota_convert_fusion.2
  5.2 0.7 bitcast_convert_fusion
  5.9 0.7 and_select_fusion.3
  6.6 0.2 convert_reduce_fusion
  6.8 0.7 multiply_add_fusion.1
  7.4 0.1 fusion.16
  7.6 0.7 compare_select_fusion.1
  8.3 0.9 broadcast_in_dim.20.meta_ref
  9.2 0.1 broadcast_multiply_fusion
  9.3 1.6 add_cosine_fusion
  10.9 1.5 fusion.waves_ref
  12.5 0.7 add_convert_fusion.pick_ref
  13.2 0.7 fusion.29.turn_ref
  13.9 0.6 broadcast_in_dim.19.unit_ref
  14.5 10.7 %fold_references.1.own_ref = bf16[40,136,128]{2,1,0:T(8,128)(2,1)} custom-call(bf16[40,2,128,128]{3,2,1,0:T(8,128)(2,1)} %bitcast.121, bf16[256,256]{1,0:T(8,128)(2,1)} %add_convert_fusion.pick_ref, bf16[128,128]{1,0:T(8,128)(2,1)} %fusion.29.turn_ref, bf16[16,128]{1,0:T(8,128)(2,1)} %broadcast_in_dim.19.unit_ref, bf16[128,512]{1,0:T(8,128)(2,1)} %fusion.waves_ref, ...), custom_call_target="tpu_custom_call" | custom-call | tf_op jit(solution)/shard_map/fold_references/pallas_call | solution.py:270
  25.2 0.2 slice_reduce_fusion.2
  25.3 0.6 broadcast_in_dim.22.nyq_ref
  25.9 0.6 fusion.4.first_ref
  26.6 111.6 %gather_sums.1 = (f32[192,8,128]{2,1,0:T(8,128)}, f32[192,8,128]{2,1,0:T(8,128)}) custom-call(s32[192]{0:T(256)} %bitcast.143, s32[192]{0:T(256)} %bitcast.142, bf16[40,136,128]{2,1,0:T(8,128)(2,1)} %fold_references.1.own_ref, bf16[128,128,128]{2,1,0:T(8,128)(2,1)} %bitcast.120, f32[3,192,128]{2,1,0:T(8,128)} %broadcast_in_dim.20.meta_ref, ...), custom_call_target="tpu_custom_call" | custom-call | tf_op jit(solution)/shard_map/gather_sums/pallas_call | solution.py:503
  138.2 1.4 copy.29
  139.6 0.0 copy-start.3
  139.6 1.2 slice.122
  140.9 1.3 copy.27
  142.2 0.9 fusion.10
  143.1 0.3 slice.126
  143.4 0.9 add_reduce_fusion
  144.3 2.0 %fusion.1 = f32[192]{0:T(256)S(1)} fusion(f32[192,8,128]{2,1,0:T(8,128)S(1)} %copy-done, f32[2,128]{1,0:T(2,128)S(1)} %add_convert_fusion.1, f32[192]{0:T(256)S(1)} %bitcast.137), kind=kLoop, calls=%fused_computation.6 | loop fusion | flops 196416 | bytes 395776 | tf_op jit(solution)/shard_map/reduce_sum | solution.py:621
  146.3 1.1 slice_reduce_fusion.1
  147.4 0.1 multiply_reduce_fusion.3
  147.6 0.1 fusion.59
  147.7 0.2 multiply_reduce_fusion.1
  147.9 0.1 multiply_reduce_fusion.2
  148.0 0.1 fusion.15
  148.2 0.0 copy-done.3
  148.2 0.2 fusion.62
  148.5 0.6 reshape.613.grad_ref
  149.1 9.3 %warp_step.1 = f32[10,512]{1,0:T(8,128)} custom-call(f32[10,512]{1,0:T(8,128)} %reshape.613.grad_ref, f32[10,512]{1,0:T(8,128)} %bitcast.129), custom_call_target="tpu_custom_call" | custom-call | tf_op jit(solution)/shard_map/warp_step/pallas_call | solution.py:553
  158.4 1.4 reshape.614
  159.7 0.6 copy.33
  (39 shorter events, 0.4 us)
Async XLA Ops:
  3.4 21.7 %copy-start.2 = (f32[2,8,2,256]{3,1,2,0:T(8,128)}, f32[2,8,2,256]{3,1,2,0:T(8,128)S(1)}, u32[]{:S(2)}) copy-start(f32[2,8,2,256]{3,1,2,0:T(8,128)S(1)} %copy.34) | copy-start | bytes 98308
  138.2 4.9 %copy-start = (f32[192,8,128]{2,1,0:T(8,128)S(1)}, f32[192,8,128]{2,1,0:T(8,128)}, u32[]{:S(2)}) copy-start(f32[192,8,128]{2,1,0:T(8,128)} %get-tuple-element.5) | copy-start | bytes 2359300
  138.2 8.1 %copy-start.1 = (f32[192,8,128]{2,1,0:T(8,128)S(1)}, f32[192,8,128]{2,1,0:T(8,128)}, u32[]{:S(2)}) copy-start(f32[192,8,128]{2,1,0:T(8,128)} %get-tuple-element.4) | copy-start | bytes 2359300
  139.6 8.5 %copy-start.3 = (s32[1,128]{1,0:T(1,128)S(1)}, s32[1,128]{1,0:T(1,128)}, u32[]{:S(2)}) copy-start(s32[1,128]{1,0:T(1,128)} %param.9) | copy-start | bytes 1540
